TPU v7x, 256 devices: a whole 4x4x8 slice. The times are simulated.
256 devices in a mesh: row: 32 (over x_lo, z, core), col: 8 (over x_hi, y).
Axes of the slice: x: 4 (x_hi: 2, x_lo: 2; x = x_hi * 2 + x_lo), y: 4, z: 8, core: 2. Of those that a mesh axis runs over, the one named last changes fastest.
Arguments:
- joined: bfloat16 [2, 32, 32, 28, 4096], P(None, None, 'row', None, 'col'), may hold values from -0.09375 to 0.09375
- probes: bfloat16 [2, 128, 4096], P(None, None, 'col'), may hold values from -6 to 6
Outputs:
- gate_rows: bfloat16 [2, 14336, 4096], P(None, 'row', 'col')
- up_rows: bfloat16 [2, 14336, 4096], P(None, 'row', 'col')
- hidden: bfloat16 [2, 128, 14336], P(None, 'col', 'row')
All inputs are finite; a program needn't handle non-finite values.
Results may differ from a plain program's by a relative error of at most 0.002.
Values may be sent and summed in bfloat16 or wider, within the bound.
No kernel may reach another device: no remote copies, remote signals or barrier semaphores. Data moves between devices by JAX's collectives and lax.ppermute only.
A program may use at most 64 MiB of HBM per device.

v0:
```python
import jax
import jax.numpy as jnp
from jax import lax
from jax.experimental import pallas as pl
from jax.experimental.pallas import tpu as pltpu
from jax.sharding import Mesh
from jax.sharding import PartitionSpec as P

ROW = ("xlo", "z", "core")
COL = ("xhi", "y")
NX, NZ, NC = 2, 8, 2
EARLY = (3, 5)
LATE = (2, 6, 1, 7)
FLIPPED = (0,) + LATE
PIECES = tuple((a, s) for s in EARLY for a in (0, 1)) + ((0, 4), (1, 4)) + tuple((1, s) for s in FLIPPED) + tuple((0, s) for s in LATE) + ((0, 0),)
PIECE = (56, 512)


def row_index(x, z, c):
    return (x * NZ + z) * NC + c


def hop(a, s, b):
    return [
        (row_index(x, z, c), row_index(x ^ a, (z + s) % NZ, c ^ b))
        for x in range(NX)
        for z in range(NZ)
        for c in range(NC)
    ]


def vmem(*shape, dtype=jnp.bfloat16):
    return pltpu.VMEM(shape, dtype)


def hbm(*shape, dtype=jnp.bfloat16):
    return pltpu.HBM(shape, dtype)


def inside(x):
    return pltpu.with_memory_space_constraint(x, pltpu.VMEM)


def outside(x):
    return pltpu.with_memory_space_constraint(x, pltpu.HBM)


WHOLE = pl.BlockSpec(memory_space=pltpu.VMEM)
ANYWHERE = pl.BlockSpec(memory_space=pl.ANY)
INHBM = pl.BlockSpec(memory_space=pltpu.HBM)


def params(mib):
    return pltpu.CompilerParams(vmem_limit_bytes=mib << 20)


def selection(pieces, row_bits):
    x, z, c = lax.axis_index("xlo"), lax.axis_index("z"), lax.axis_index("core")
    row = lax.broadcasted_iota(jnp.int32, (16 * len(pieces), 256), 0)
    column = lax.broadcasted_iota(jnp.int32, (16 * len(pieces), 256), 1)
    j, b, n = row & 7, (row >> 3) & 1, row >> 4
    flip, step = jnp.zeros_like(n), jnp.zeros_like(n)
    for i, (a, s) in enumerate(pieces):
        flip = jnp.where(n == i, a, flip)
        step = jnp.where(n == i, s, step)
    block = ((flip ^ x) << 4) + (((z + step) & 7) << 1) + (b ^ c)
    return (column == (j << row_bits) + block).astype(jnp.bfloat16)


def pack_first_kernel(w_hbm, *refs):
    outs, w, sems = refs[:2], refs[2], refs[3]
    copies = [pltpu.make_async_copy(w_hbm.at[pl.ds(8 * g, 8)], w.at[pl.ds(8 * g, 8)], sems.at[g]) for g in range(7)]
    for copy in copies:
        copy.start()
    pick = selection(PIECES[:4], 5)
    for g in range(7):
        copies[g].wait()
        rows = w[8 * g : 8 * g + 8].reshape(256, 512)
        moved = jnp.dot(pick, rows, preferred_element_type=jnp.float32).astype(jnp.bfloat16)
        moved = moved.reshape(2, 2, 2, 8, 512)
        for i in range(2):
            outs[i][:, :, 8 * g : 8 * g + 8, :] = moved[i]


def pack_first(w):
    return pl.pallas_call(
        pack_first_kernel,
        out_shape=[vmem(2, 2, *PIECE)] * 2 + [vmem(56, 32, 512)],
        in_specs=[INHBM],
        out_specs=[WHOLE] * 3,
        scratch_shapes=[pltpu.SemaphoreType.DMA((7,))],
        compiler_params=params(4),
        name="pack_first",
    )(outside(w))


def pack_second_kernel(w, probes_hbm, *refs):
    outs, parts, (held, probes, proj, sems, out_sems, part_sems) = refs[:8], refs[8:12], refs[12:]
    y = lax.axis_index("y")
    first = pltpu.make_async_copy(probes_hbm, probes, sems.at[0])
    first.start()
    pick = selection(PIECES[4:], 5)
    dims = (((1,), (1,)), ((), ()))
    sent = []

    def ship(half, begin, count):
        rows = pl.ds(begin, count)
        pairs = [(held.at[i, :, rows], outs[i].at[:, rows]) for i in range(2)]
        pairs.append((held.at[pl.ds(2, 5), :, rows], outs[2].at[:, :, rows]))
        pairs += [(held.at[7 + i, :, rows], outs[3 + i].at[0, :, rows]) for i in range(4)]
        pairs.append((held.at[11, :, rows], outs[7].at[:, rows]))
        for i, (source, target) in enumerate(pairs):
            sent.append(pltpu.make_async_copy(source, target, out_sems.at[8 * half + i]))
            sent[-1].start()

    for layer in range(2):
        part = w[28 * layer : 28 * layer + 28].reshape(896, 512)
        if layer == 0:
            first.wait()
        product = lax.dot_general(probes[layer], part, dims, preferred_element_type=jnp.float32)
        proj[layer] = product.reshape(8, 16, 896)
        for s in range(1, 4):
            for h in range(2):
                n = len(sent)
                source = proj.at[layer, 4 * h + ((y + s) & 3)]
                sent.append(pltpu.make_async_copy(source, parts[s].at[h, layer], part_sems.at[n]))
                sent[-1].start()
        for h in range(2):
            parts[0][h, layer] = proj[layer, 4 * h + y]
    for g in range(7):
        rows = w[8 * g : 8 * g + 8].reshape(256, 512)
        moved = jnp.dot(pick, rows, preferred_element_type=jnp.float32).astype(jnp.bfloat16)
        held[:, :, 8 * g : 8 * g + 8, :] = moved.reshape(12, 2, 8, 512)
        if g == 3:
            ship(0, 0, 32)
    ship(1, 32, 24)
    for copy in sent:
        copy.wait()


def pack_second(w, probes):
    return pl.pallas_call(
        pack_second_kernel,
        out_shape=[hbm(2, *PIECE)] * 2
        + [hbm(5, 2, *PIECE)]
        + [hbm(2, 2, *PIECE)] * 4
        + [hbm(2, *PIECE)]
        + [vmem(2, 2, 16, 896, dtype=jnp.float32)]
        + [hbm(2, 2, 16, 896, dtype=jnp.float32)] * 3,
        in_specs=[WHOLE, INHBM],
        out_specs=[INHBM] * 8 + [WHOLE] + [INHBM] * 3,
        scratch_shapes=[
            pltpu.VMEM((12, 2, 56, 512), jnp.bfloat16),
            pltpu.VMEM((2, 128, 512), jnp.bfloat16),
            pltpu.VMEM((2, 8, 16, 896), jnp.float32),
            pltpu.SemaphoreType.DMA((1,)),
            pltpu.SemaphoreType.DMA((16,)),
            pltpu.SemaphoreType.DMA((12,)),
        ],
        compiler_params=params(8),
        name="pack_second",
    )(inside(w), outside(probes))


def join_kernel(crossed, *refs):
    outs, sems = refs[4:8], refs[8]
    copies = [pltpu.make_async_copy(crossed.at[1 + n], out.at[1], sems.at[n]) for n, out in enumerate(outs)]
    for copy in copies:
        copy.start()
    for copy in copies:
        copy.wait()


def join(crossed, straight):
    return pl.pallas_call(
        join_kernel,
        out_shape=[hbm(2, 2, *PIECE)] * 4,
        in_specs=[WHOLE] + [INHBM] * 4,
        out_specs=[INHBM] * 4,
        scratch_shapes=[pltpu.SemaphoreType.DMA((4,))],
        input_output_aliases={1: 0, 2: 1, 3: 2, 4: 3},
        compiler_params=params(1),
        name="join",
    )(inside(crossed), *map(outside, straight))


def gather_kernel(*refs):
    pieces, out, sems = refs[:2], refs[2], refs[3]
    copies = [pltpu.make_async_copy(piece.at[1], out.at[n], sems.at[n]) for n, piece in enumerate(pieces)]
    for copy in copies:
        copy.start()
    for copy in copies:
        copy.wait()


def gather(pieces):
    return pl.pallas_call(
        gather_kernel,
        out_shape=vmem(2, 2, *PIECE),
        in_specs=[ANYWHERE] * 2,
        out_specs=WHOLE,
        scratch_shapes=[pltpu.SemaphoreType.DMA((2,))],
        compiler_params=params(1),
        name="gather",
    )(*pieces)


def unpack_kernel(*refs):
    early, late, (gate_hbm, up_hbm, held, rows_out, sems, out_sems) = refs[:14], refs[14:22], refs[22:]
    x, z, c = lax.axis_index("xlo"), lax.axis_index("z"), lax.axis_index("core")
    local, crossed, z3, z5, d04, d14, post = early[0:2], early[2:4], early[4:6], early[6:8], early[8:10], early[10:12], early[12:14]
    pieces = []
    for b in range(2):
        pieces += [(local[b].at[b], 0, 0, b), (crossed[b].at[0, b], 1, 0, b)]
        pieces += [(z3[b].at[0, b], 0, 3, b), (post[b].at[0, b], 1, 3, b)]
        pieces += [(z5[b].at[0, b], 0, 5, b), (post[b].at[1, b], 1, 5, b)]
        pieces += [(d04[b].at[b], 0, 4, b), (d14[b].at[b], 1, 4, b)]

    def place(a, s, b):
        return (a ^ x) * 4 + (((z - s) & 7) >> 1), (z - s) & 1, b ^ c

    copies = []
    for source, a, s, b in pieces:
        copies.append(pltpu.make_async_copy(source, held.at[place(a, s, b)], sems.at[len(copies)]))
        copies[-1].start()
    out = lax.broadcasted_iota(jnp.int32, (224, 224), 0)
    inn = lax.broadcasted_iota(jnp.int32, (224, 224), 1)
    source = jnp.zeros((224, 224), jnp.int32)
    for q in range(4):
        for layer in range(2):
            for g in range(2):
                first = (layer * 2 + g) * 56 + q * 14
                here = (out >= first) & (out < first + 14)
                source = jnp.where(here, q * 56 + layer * 28 + g + 2 * (out - first), source)
    pick = (inn == source).astype(jnp.bfloat16)
    for i, s in enumerate(LATE):
        for a in range(2):
            for b in range(2):
                held[place(a, s, b)] = late[2 * i + b][a, b]
    for copy in copies:
        copy.wait()
    copies = []
    for n in range(8):
        rows = held[n].reshape(224, 512)
        moved = jnp.dot(pick, rows, preferred_element_type=jnp.float32).astype(jnp.bfloat16)
        for layer in range(2):
            for g in range(2):
                first = (layer * 2 + g) * 56
                rows_out[n, g, layer] = moved[first : first + 56]
        for g, target in enumerate((gate_hbm, up_hbm)):
            copy = pltpu.make_async_copy(rows_out.at[n, g], target.at[:, pl.ds(56 * n, 56)], out_sems.at[2 * n + g])
            copy.start()
            copies.append(copy)
    for copy in copies:
        copy.wait()


def unpack(early, late):
    return pl.pallas_call(
        unpack_kernel,
        out_shape=[hbm(2, 448, 512)] * 2,
        in_specs=[INHBM] * 2 + [ANYWHERE] * 2 + [INHBM] * 10 + [WHOLE] * 8,
        out_specs=[INHBM] * 2,
        scratch_shapes=[
            pltpu.VMEM((8, 2, 2, 56, 512), jnp.bfloat16),
            pltpu.VMEM((8, 2, 2, 56, 512), jnp.bfloat16),
            pltpu.SemaphoreType.DMA((16,)),
            pltpu.SemaphoreType.DMA((16,)),
        ],
        compiler_params=params(10),
        name="unpack",
    )(*map(outside, early[:2]), *early[2:4], *map(outside, early[4:]), *map(inside, late))


def halve_kernel(p0, p1, p2, p3, keep, give):
    h = lax.axis_index("xhi")
    keep[...] = (p0[h] + p1[h]) + (p2[h] + p3[h])
    give[...] = (p0[1 - h] + p1[1 - h]) + (p2[1 - h] + p3[1 - h])


def halve(parts):
    return pl.pallas_call(
        halve_kernel,
        out_shape=[vmem(2, 16, 896, dtype=jnp.float32)] * 2,
        in_specs=[WHOLE] * 4,
        out_specs=[WHOLE] * 2,
        compiler_params=params(8),
        name="halve",
    )(inside(parts[0]), *parts[1:])


def gated_kernel(keep, came, out_ref):
    total = (keep[...] + came[...]).reshape(32, 896)
    up = pltpu.roll(total, 896 - 32, 1)
    turned = (total / (1.0 + jnp.exp(-total)) * up).T
    quads = []
    for q in range(4):
        blocks = [turned[64 * i : 64 * i + 32] if i < 14 else jnp.zeros((32, 32), jnp.float32) for i in range(4 * q, 4 * q + 4)]
        quads.append(jnp.concatenate(blocks, axis=1))
    rows = jnp.concatenate(quads, axis=0).astype(jnp.bfloat16)
    to = lax.broadcasted_iota(jnp.int32, (128, 128), 0)
    of = lax.broadcasted_iota(jnp.int32, (128, 128), 1)
    pick = (of == ((to & 3) << 5) + (to >> 2)).astype(jnp.bfloat16)
    out_ref[...] = jnp.dot(pick, rows, preferred_element_type=jnp.float32).astype(jnp.bfloat16)


def gated(keep, came):
    return pl.pallas_call(
        gated_kernel,
        out_shape=jax.ShapeDtypeStruct((128, 128), jnp.bfloat16),
        in_specs=[WHOLE] * 2,
        out_specs=WHOLE,
        compiler_params=params(8),
        name="gated",
    )(inside(keep), inside(came))


def final_kernel(came, out_ref):
    turned = came[...].astype(jnp.float32).T.astype(jnp.bfloat16)
    of = lax.broadcasted_iota(jnp.int32, (128, 448), 0)
    to = lax.broadcasted_iota(jnp.int32, (128, 448), 1)
    total = jnp.zeros((32, 448), jnp.float32)
    for i in range(4):
        unit = ((of & 3) << 2) + i
        pick = ((to == (of >> 2) * 14 + unit) & (unit < 14)).astype(jnp.bfloat16)
        total += jnp.dot(turned[32 * i : 32 * i + 32], pick, preferred_element_type=jnp.float32)
    out_ref[...] = total.astype(jnp.bfloat16).reshape(2, 16, 448)


def final(came):
    return pl.pallas_call(
        final_kernel,
        out_shape=jax.ShapeDtypeStruct((2, 16, 448), jnp.bfloat16),
        in_specs=[WHOLE],
        out_specs=WHOLE,
        compiler_params=params(8),
        name="final",
    )(came)


def send(piece, a, s, b):
    return lax.ppermute(piece, ROW, hop(a, s, b))


def side(piece, h, y):
    pairs = [(p * 4 + q, (p ^ h) * 4 + (q + y) % 4) for p in range(2) for q in range(4)]
    return lax.ppermute(piece, COL, pairs)


def body(joined, probes):
    w = joined.reshape(2, 32, 28, 512).transpose(0, 2, 1, 3).reshape(56, 32, 512)
    *outs, w = pack_first(w)
    rest = pack_second(w, probes)
    outs, parts = [*outs, *rest[:8]], rest[8:]
    early = [send(piece, 0, s, 0) for s, piece in zip(EARLY, outs)]
    across = [send(piece, a, 4, 0) for a, piece in zip((0, 1), outs[2:4])]
    crossed = send(outs[4], 1, 0, 0)
    parts = [parts[0]] + [side(parts[s], 0, s) for s in range(1, 4)]
    keep, give = halve(parts)
    came = side(give, 1, 0)
    joins = join(crossed, outs[5:9])
    late = [send(piece, 0, s, 0) for s, piece in zip(LATE, joins)]
    post = gather(early)
    post = send(post, 1, 0, 0)
    mine = early + across + [post, crossed] + late + [outs[9]]
    other = [send(piece, 0, 0, 1) for piece in mine]
    hid = gated(keep, came).reshape(32, 4, 128)
    hid = lax.all_to_all(hid, ROW, 0, 0, tiled=True)
    hid = final(hid.reshape(128, 128))
    both = [piece for pair in zip(mine, other) for piece in pair]
    gate_rows, up_rows = unpack(both[20:22] + both[10:12] + both[0:10], both[12:20])
    return gate_rows, up_rows, hid


def solution(mesh):
    split = Mesh(mesh.devices.reshape(NX, NZ, NC, 2, 4), ROW + COL)
    return jax.shard_map(
        body,
        mesh=split,
        in_specs=(P(None, None, ROW, None, COL), P(None, None, COL)),
        out_specs=(P(None, ROW, COL), P(None, ROW, COL), P(None, COL, ROW)),
        check_vma=False,
    )
```

profile of v0, /device:TPU:1, one launch (start us, length us, event | category | flops | bytes accessed | tf_op | source)
XLA Modules:
  0.0 104.1 jit_solution(1603125808776893367)
XLA Ops:
  0.6 2.2 %pack_first.1 = (bf16[2,2,56,512]{3,2,1,0:T(8,128)(2,1)S(1)}, bf16[2,2,56,512]{3,2,1,0:T(8,128)(2,1)S(1)}, bf16[56,32,512]{2,1,0:T(8,128)(2,1)S(1)}) custom-call(bf16[56,32,512]{2,1,0:T(8,128)(2,1)} %bitcast.9), custom_call_target="tpu_custom_call" | custom-call | tf_op jit(solution)/shard_map/pack_first/pallas_call | solution.py:86
  2.8 3.3 %pack_second.1 = (bf16[2,56,512]{2,1,0:T(8,128)(2,1)}, bf16[2,56,512]{2,1,0:T(8,128)(2,1)}, bf16[5,2,56,512]{3,2,1,0:T(8,128)(2,1)}, bf16[2,2,56,512]{3,2,1,0:T(...) custom-call(bf16[56,32,512]{2,1,0:T(8,128)(2,1)S(1)} %get-tuple-elem, ...), custom_call_target="tpu_custom_call" | custom-call | tf_op jit(solution)/shard_map/pack_second/pallas_call | solution.py:142
  6.1 7.8 %collective-permute-start.7 = (bf16[2,56,512]{2,1,0:T(8,128)(2,1)}, bf16[2,56,512]{2,1,0:T(8,128)(2,1)S(1)}, u32[]{:S(2)}, u32[]{:S(2)}) collective-permute-start(bf16[2,56,512]{2,1,0:T(8,128)(2,1)} %get-tuple-element.31), channel_id=1, source_target_pairs={{0,64},{8,72},{16,80},{24,88},{32,96},{40,104},{48,112},{56,120},{... | collective-permute-start | bytes 344072 | tf_op jit(solution)/shard_map/ppermute | solution.py:342
  13.9 1.6 %collective-permute-start.3 = (bf16[2,2,56,512]{3,2,1,0:T(8,128)(2,1)S(1)}, bf16[2,2,56,512]{3,2,1,0:T(8,128)(2,1)S(1)}, u32[]{:S(2)}, u32[]{:S(2)}) collective-permute-start(bf16[2,2,56,512]{3,2,1,0:T(8,128)(2,1)S(1)} %get-tuple-element.29), channel_id=1, source_target_pairs={{0,48},{8,56},{16,64},{24,72},{32,80},{40,88},{48,96},{56,104},{64... | collective-permute-start | bytes 688136 | tf_op jit(solution)/shard_map/ppermute | solution.py:342
  15.6 2.8 %collective-permute-start.5 = (bf16[2,2,56,512]{3,2,1,0:T(8,128)(2,1)S(1)}, bf16[2,2,56,512]{3,2,1,0:T(8,128)(2,1)S(1)}, u32[]{:S(2)}, u32[]{:S(2)}) collective-permute-start(bf16[2,2,56,512]{3,2,1,0:T(8,128)(2,1)S(1)} %get-tuple-element.30), channel_id=1, source_target_pairs={{0,80},{8,88},{16,96},{24,104},{32,112},{40,120},{48,0},{56,8},{64... | collective-permute-start | bytes 688136 | tf_op jit(solution)/shard_map/ppermute | solution.py:342
  18.4 1.4 %collective-permute-start.9 = (bf16[2,56,512]{2,1,0:T(8,128)(2,1)}, bf16[2,56,512]{2,1,0:T(8,128)(2,1)S(1)}, u32[]{:S(2)}, u32[]{:S(2)}) collective-permute-start(bf16[2,56,512]{2,1,0:T(8,128)(2,1)} %get-tuple-element.32), channel_id=1, source_target_pairs={{0,192},{8,200},{16,208},{24,216},{32,224},{40,232},{48,240},{56,2... | collective-permute-start | bytes 344072 | tf_op jit(solution)/shard_map/ppermute | solution.py:342
  19.8 0.2 collective-permute-start.1
  20.1 0.0 collective-permute-done.7.refs_8_
  20.1 1.8 %collective-permute-start = (bf16[2,56,512]{2,1,0:T(8,128)(2,1)}, bf16[2,56,512]{2,1,0:T(8,128)(2,1)S(1)}, u32[]{:S(2)}, u32[]{:S(2)}) collective-permute-start(bf16[2,56,512]{2,1,0:T(8,128)(2,1)} %get-tuple-element.27.refs_0_), channel_id=1, source_target_pairs={{0,8},{8,0},{16,24},{24,16},{32,40},{40,32},{48,56},{56,48},{64,72... | collective-permute-start | bytes 344072 | tf_op jit(solution)/shard_map/ppermute | solution.py:342
  21.9 14.7 %collective-permute-done.9.refs_10_ = bf16[2,56,512]{2,1,0:T(8,128)(2,1)S(1)} collective-permute-done((bf16[2,56,512]{2,1,0:T(8,128)(2,1)}, bf16[2,56,512]{2,1,0:T(8,128)(2,1)S(1)}, u32[]{:S(2)}, u32[]{:S(2)}) %collective-permute-start.9) | collective-permute-done | bytes 114720 | tf_op jit(solution)/shard_map/ppermute | solution.py:342
  36.6 1.6 %collective-permute-start.8 = (bf16[2,56,512]{2,1,0:T(8,128)(2,1)S(1)}, bf16[2,56,512]{2,1,0:T(8,128)(2,1)S(1)}, u32[]{:S(2)}, u32[]{:S(2)}) collective-permute-start(bf16[2,56,512]{2,1,0:T(8,128)(2,1)S(1)} %collective-permute-done.7.refs_8_), channel_id=1, source_target_pairs={{0,8},{8,0},{16,24},{24,16},{32,40},{40,32},{48,56},{56,48},{64,72... | collective-permute-start | bytes 344072 | tf_op jit(solution)/shard_map/ppermute | solution.py:342
  38.2 0.0 collective-permute-done.refs_1_
  38.2 1.3 %collective-permute-start.21 = (f32[2,2,16,896]{3,2,1,0:T(8,128)}, f32[2,2,16,896]{3,2,1,0:T(8,128)S(1)}, u32[]{:S(2)}, u32[]{:S(2)}) collective-permute-start(f32[2,2,16,896]{3,2,1,0:T(8,128)} %get-tuple-element.44), channel_id=1, source_target_pairs={{0,1},{1,2},{2,3},{3,0},{4,5},{5,6},{6,7},{7,4},{8,9},{9,10},{10,1... | collective-permute-start | bytes 688136 | tf_op jit(solution)/shard_map/ppermute | solution.py:347
  39.5 2.6 %collective-permute-start.22 = (f32[2,2,16,896]{3,2,1,0:T(8,128)}, f32[2,2,16,896]{3,2,1,0:T(8,128)S(1)}, u32[]{:S(2)}, u32[]{:S(2)}) collective-permute-start(f32[2,2,16,896]{3,2,1,0:T(8,128)} %get-tuple-element.45), channel_id=1, source_target_pairs={{0,2},{1,3},{2,0},{3,1},{4,6},{5,7},{6,4},{7,5},{8,10},{9,11},{10,... | collective-permute-start | bytes 688136 | tf_op jit(solution)/shard_map/ppermute | solution.py:347
  42.2 0.0 collective-permute-done.5.refs_1_.refs_6_
  42.2 1.1 %collective-permute-start.23 = (f32[2,2,16,896]{3,2,1,0:T(8,128)}, f32[2,2,16,896]{3,2,1,0:T(8,128)S(1)}, u32[]{:S(2)}, u32[]{:S(2)}) collective-permute-start(f32[2,2,16,896]{3,2,1,0:T(8,128)} %get-tuple-element.46), channel_id=1, source_target_pairs={{0,3},{1,0},{2,1},{3,2},{4,7},{5,4},{6,5},{7,6},{8,11},{9,8},{10,9... | collective-permute-start | bytes 688136 | tf_op jit(solution)/shard_map/ppermute | solution.py:347
  43.2 0.3 gather.1
  43.5 0.0 collective-permute-done.8.refs_9_
  43.5 0.3 collective-permute-start.11
  43.9 3.0 %collective-permute-done.21.p1 = f32[2,2,16,896]{3,2,1,0:T(8,128)S(1)} collective-permute-done((f32[2,2,16,896]{3,2,1,0:T(8,128)}, f32[2,2,16,896]{3,2,1,0:T(8,128)S(1)}, u32[]{:S(2)}, u32[]{:S(2)}) %collective-permute-start.21) | collective-permute-done | bytes 229408 | tf_op jit(solution)/shard_map/ppermute | solution.py:347
  46.9 0.9 collective-permute-start.10
  47.7 5.1 %collective-permute-done.22.p2 = f32[2,2,16,896]{3,2,1,0:T(8,128)S(1)} collective-permute-done((f32[2,2,16,896]{3,2,1,0:T(8,128)}, f32[2,2,16,896]{3,2,1,0:T(8,128)S(1)}, u32[]{:S(2)}, u32[]{:S(2)}) %collective-permute-start.22) | collective-permute-done | bytes 229408 | tf_op jit(solution)/shard_map/ppermute | solution.py:347
  52.9 0.9 collective-permute-start.4
  53.8 0.0 collective-permute-done.23.p3
  53.8 0.0 collective-permute-start.6
  53.8 0.0 collective-permute-done.11.refs_12_
  53.9 0.5 collective-permute-start.12
  54.4 0.0 collective-permute-done.10.refs_11_
  54.4 2.5 %collective-permute-start.24 = (f32[2,16,896]{2,1,0:T(8,128)S(1)}, f32[2,16,896]{2,1,0:T(8,128)S(1)}, u32[]{:S(2)}, u32[]{:S(2)}) collective-permute-start(f32[2,16,896]{2,1,0:T(8,128)S(1)} %get-tuple-element.48), channel_id=1, source_target_pairs={{0,4},{1,5},{2,6},{3,7},{4,0},{5,1},{6,2},{7,3},{8,12},{9,13},{10,... | collective-permute-start | bytes 344072 | tf_op jit(solution)/shard_map/ppermute | solution.py:347
  57.0 0.0 collective-permute-done.1.crossed.refs_2_
  57.0 0.4 collective-permute-start.2
  57.4 0.8 join.1
  58.2 2.5 %collective-permute-done.24.came = f32[2,16,896]{2,1,0:T(8,128)S(1)} collective-permute-done((f32[2,16,896]{2,1,0:T(8,128)S(1)}, f32[2,16,896]{2,1,0:T(8,128)S(1)}, u32[]{:S(2)}, u32[]{:S(2)}) %collective-permute-start.24) | collective-permute-done | bytes 114720 | tf_op jit(solution)/shard_map/ppermute | solution.py:347
  60.6 4.5 %collective-permute-start.13 = (bf16[2,2,56,512]{3,2,1,0:T(8,128)(2,1)}, bf16[2,2,56,512]{3,2,1,0:T(8,128)(2,1)S(1)}, u32[]{:S(2)}, u32[]{:S(2)}) collective-permute-start(bf16[2,2,56,512]{3,2,1,0:T(8,128)(2,1)} %get-tuple-element.37), channel_id=1, source_target_pairs={{0,32},{8,40},{16,48},{24,56},{32,64},{40,72},{48,80},{56,88},{64,... | collective-permute-start | bytes 688136 | tf_op jit(solution)/shard_map/ppermute | solution.py:342
  65.2 3.2 %collective-permute-start.15 = (bf16[2,2,56,512]{3,2,1,0:T(8,128)(2,1)}, bf16[2,2,56,512]{3,2,1,0:T(8,128)(2,1)S(1)}, u32[]{:S(2)}, u32[]{:S(2)}) collective-permute-start(bf16[2,2,56,512]{3,2,1,0:T(8,128)(2,1)} %get-tuple-element.38), channel_id=1, source_target_pairs={{0,96},{8,104},{16,112},{24,120},{32,0},{40,8},{48,16},{56,24},{64... | collective-permute-start | bytes 688136 | tf_op jit(solution)/shard_map/ppermute | solution.py:342
  68.3 0.0 collective-permute-done.6.refs_7_
  68.4 2.7 %collective-permute-start.19 = (bf16[2,2,56,512]{3,2,1,0:T(8,128)(2,1)}, bf16[2,2,56,512]{3,2,1,0:T(8,128)(2,1)S(1)}, u32[]{:S(2)}, u32[]{:S(2)}) collective-permute-start(bf16[2,2,56,512]{3,2,1,0:T(8,128)(2,1)} %get-tuple-element.40), channel_id=1, source_target_pairs={{0,112},{8,120},{16,0},{24,8},{32,16},{40,24},{48,32},{56,40},{64,... | collective-permute-start | bytes 688136 | tf_op jit(solution)/shard_map/ppermute | solution.py:342
  71.0 7.5 %collective-permute-done.13.refs_14_ = bf16[2,2,56,512]{3,2,1,0:T(8,128)(2,1)S(1)} collective-permute-done((bf16[2,2,56,512]{3,2,1,0:T(8,128)(2,1)}, bf16[2,2,56,512]{3,2,1,0:T(8,128)(2,1)S(1)}, u32[]{:S(2)}, u32[]{:S(2)}) %collective-permute-start.13) | collective-permute-done | bytes 229408 | tf_op jit(solution)/shard_map/ppermute | solution.py:342
  78.5 1.8 %collective-permute-start.14 = (bf16[2,2,56,512]{3,2,1,0:T(8,128)(2,1)S(1)}, bf16[2,2,56,512]{3,2,1,0:T(8,128)(2,1)S(1)}, u32[]{:S(2)}, u32[]{:S(2)}) collective-permute-start(bf16[2,2,56,512]{3,2,1,0:T(8,128)(2,1)S(1)} %collective-permute-done.13.refs_14_), channel_id=1, source_target_pairs={{0,8},{8,0},{16,24},{24,16},{32,40},{40,32},{48,56},{56,48},{64,72... | collective-permute-start | bytes 688136 | tf_op jit(solution)/shard_map/ppermute | solution.py:342
  80.3 0.4 collective-permute-start.16
  80.7 0.9 collective-permute-done.17.refs_18_
  81.6 1.5 %collective-permute-start.18 = (bf16[2,2,56,512]{3,2,1,0:T(8,128)(2,1)S(1)}, bf16[2,2,56,512]{3,2,1,0:T(8,128)(2,1)S(1)}, u32[]{:S(2)}, u32[]{:S(2)}) collective-permute-start(bf16[2,2,56,512]{3,2,1,0:T(8,128)(2,1)S(1)} %collective-permute-done.17.refs_18_), channel_id=1, source_target_pairs={{0,8},{8,0},{16,24},{24,16},{32,40},{40,32},{48,56},{56,48},{64,72... | collective-permute-start | bytes 688136 | tf_op jit(solution)/shard_map/ppermute | solution.py:342
  83.2 0.5 collective-permute-done.19.refs_20_
  83.6 0.6 collective-permute-start.20
  84.2 0.4 gated.1
  84.6 15.3 %all_to_all.5 = bf16[32,4,128]{2,1,0:T(4,128)(2,1)S(1)} all-to-all(bf16[32,4,128]{2,1,0:T(4,128)(2,1)S(1)} %bitcast.8), channel_id=1, replica_groups=mesh['xlo'=2,'z'=8,'core'=2,'xhi'=2,'y'=4] {'xlo','z','core'}, dimensions={0} | all-to-all | bytes 65536 | tf_op jit(solution)/shard_map/all_to_all | solution.py:368
  99.9 0.9 final.1
  101.0 3.0 %unpack.1 = (bf16[2,448,512]{2,1,0:T(8,128)(2,1)}, bf16[2,448,512]{2,1,0:T(8,128)(2,1)}) custom-call(bf16[2,56,512]{2,1,0:T(8,128)(2,1)} %get-tuple-element.27.refs_0_, bf16[2,56,512]{2,1,0:T(8,128)(2,1)} %copy-done.8, bf16[5,2,56,512]{3,2,1,0:T(8,128)(2,1)S(1)} %collective-permute-done.1.crossed.refs_2_, ...), custom_call_target="tpu_custom_call" | custom-call | tf_op jit(solution)/shard_map/unpack/pallas_call | solution.py:259
  (33 shorter events, 0.1 us)
Async XLA Ops:
  6.1 13.9 %collective-permute-start.7 = (bf16[2,56,512]{2,1,0:T(8,128)(2,1)}, bf16[2,56,512]{2,1,0:T(8,128)(2,1)S(1)}, u32[]{:S(2)}, u32[]{:S(2)}) collective-permute-start(bf16[2,56,512]{2,1,0:T(8,128)(2,1)} %get-tuple-element.31), channel_id=1, source_target_pairs={{0,64},{8,72},{16,80},{24,88},{32,96},{40,104},{48,112},{56,120},{... | collective-permute-start | bytes 344072 | tf_op jit(solution)/shard_map/ppermute | solution.py:342
  13.9 25.6 %collective-permute-start.3 = (bf16[2,2,56,512]{3,2,1,0:T(8,128)(2,1)S(1)}, bf16[2,2,56,512]{3,2,1,0:T(8,128)(2,1)S(1)}, u32[]{:S(2)}, u32[]{:S(2)}) collective-permute-start(bf16[2,2,56,512]{3,2,1,0:T(8,128)(2,1)S(1)} %get-tuple-element.29), channel_id=1, source_target_pairs={{0,48},{8,56},{16,64},{24,72},{32,80},{40,88},{48,96},{56,104},{64... | collective-permute-start | bytes 688136 | tf_op jit(solution)/shard_map/ppermute | solution.py:342
  15.6 26.6 %collective-permute-start.5 = (bf16[2,2,56,512]{3,2,1,0:T(8,128)(2,1)S(1)}, bf16[2,2,56,512]{3,2,1,0:T(8,128)(2,1)S(1)}, u32[]{:S(2)}, u32[]{:S(2)}) collective-permute-start(bf16[2,2,56,512]{3,2,1,0:T(8,128)(2,1)S(1)} %get-tuple-element.30), channel_id=1, source_target_pairs={{0,80},{8,88},{16,96},{24,104},{32,112},{40,120},{48,0},{56,8},{64... | collective-permute-start | bytes 688136 | tf_op jit(solution)/shard_map/ppermute | solution.py:342
  18.4 18.2 %collective-permute-start.9 = (bf16[2,56,512]{2,1,0:T(8,128)(2,1)}, bf16[2,56,512]{2,1,0:T(8,128)(2,1)S(1)}, u32[]{:S(2)}, u32[]{:S(2)}) collective-permute-start(bf16[2,56,512]{2,1,0:T(8,128)(2,1)} %get-tuple-element.32), channel_id=1, source_target_pairs={{0,192},{8,200},{16,208},{24,216},{32,224},{40,232},{48,240},{56,2... | collective-permute-start | bytes 344072 | tf_op jit(solution)/shard_map/ppermute | solution.py:342
  19.8 37.2 %collective-permute-start.1 = (bf16[5,2,56,512]{3,2,1,0:T(8,128)(2,1)}, bf16[5,2,56,512]{3,2,1,0:T(8,128)(2,1)S(1)}, u32[]{:S(2)}, u32[]{:S(2)}) collective-permute-start(bf16[5,2,56,512]{3,2,1,0:T(8,128)(2,1)} %get-tuple-element.28), channel_id=1, source_target_pairs={{0,128},{8,136},{16,144},{24,152},{32,160},{40,168},{48,176},{56,1... | collective-permute-start | bytes 1720328 | tf_op jit(solution)/shard_map/ppermute | solution.py:342
  20.1 80.8 %copy-start.6 = (bf16[2,56,512]{2,1,0:T(8,128)(2,1)}, bf16[2,56,512]{2,1,0:T(8,128)(2,1)S(1)}, u32[]{:S(2)}) copy-start(bf16[2,56,512]{2,1,0:T(8,128)(2,1)S(1)} %collective-permute-done.7.refs_8_) | copy-start | bytes 344068
  20.1 18.2 %collective-permute-start = (bf16[2,56,512]{2,1,0:T(8,128)(2,1)}, bf16[2,56,512]{2,1,0:T(8,128)(2,1)S(1)}, u32[]{:S(2)}, u32[]{:S(2)}) collective-permute-start(bf16[2,56,512]{2,1,0:T(8,128)(2,1)} %get-tuple-element.27.refs_0_), channel_id=1, source_target_pairs={{0,8},{8,0},{16,24},{24,16},{32,40},{40,32},{48,56},{56,48},{64,72... | collective-permute-start | bytes 344072 | tf_op jit(solution)/shard_map/ppermute | solution.py:342
  36.6 64.3 %copy-start.7 = (bf16[2,56,512]{2,1,0:T(8,128)(2,1)}, bf16[2,56,512]{2,1,0:T(8,128)(2,1)S(1)}, u32[]{:S(2)}) copy-start(bf16[2,56,512]{2,1,0:T(8,128)(2,1)S(1)} %collective-permute-done.9.refs_10_) | copy-start | bytes 344068
  36.6 6.9 %collective-permute-start.8 = (bf16[2,56,512]{2,1,0:T(8,128)(2,1)S(1)}, bf16[2,56,512]{2,1,0:T(8,128)(2,1)S(1)}, u32[]{:S(2)}, u32[]{:S(2)}) collective-permute-start(bf16[2,56,512]{2,1,0:T(8,128)(2,1)S(1)} %collective-permute-done.7.refs_8_), channel_id=1, source_target_pairs={{0,8},{8,0},{16,24},{24,16},{32,40},{40,32},{48,56},{56,48},{64,72... | collective-permute-start | bytes 344072 | tf_op jit(solution)/shard_map/ppermute | solution.py:342
  38.2 62.6 %copy-start.8 = (bf16[2,56,512]{2,1,0:T(8,128)(2,1)}, bf16[2,56,512]{2,1,0:T(8,128)(2,1)S(1)}, u32[]{:S(2)}) copy-start(bf16[2,56,512]{2,1,0:T(8,128)(2,1)S(1)} %collective-permute-done.refs_1_) | copy-start | bytes 344068
  38.2 8.6 %collective-permute-start.21 = (f32[2,2,16,896]{3,2,1,0:T(8,128)}, f32[2,2,16,896]{3,2,1,0:T(8,128)S(1)}, u32[]{:S(2)}, u32[]{:S(2)}) collective-permute-start(f32[2,2,16,896]{3,2,1,0:T(8,128)} %get-tuple-element.44), channel_id=1, source_target_pairs={{0,1},{1,2},{2,3},{3,0},{4,5},{5,6},{6,7},{7,4},{8,9},{9,10},{10,1... | collective-permute-start | bytes 688136 | tf_op jit(solution)/shard_map/ppermute | solution.py:347
  39.5 61.3 %copy-start = (bf16[2,2,56,512]{3,2,1,0:T(8,128)(2,1)}, bf16[2,2,56,512]{3,2,1,0:T(8,128)(2,1)S(1)}, u32[]{:S(2)}) copy-start(bf16[2,2,56,512]{3,2,1,0:T(8,128)(2,1)S(1)} %collective-permute-done.3.refs_0_.refs_4_) | copy-start | bytes 688132
  39.5 13.3 %collective-permute-start.22 = (f32[2,2,16,896]{3,2,1,0:T(8,128)}, f32[2,2,16,896]{3,2,1,0:T(8,128)S(1)}, u32[]{:S(2)}, u32[]{:S(2)}) collective-permute-start(f32[2,2,16,896]{3,2,1,0:T(8,128)} %get-tuple-element.45), channel_id=1, source_target_pairs={{0,2},{1,3},{2,0},{3,1},{4,6},{5,7},{6,4},{7,5},{8,10},{9,11},{10,... | collective-permute-start | bytes 688136 | tf_op jit(solution)/shard_map/ppermute | solution.py:347
  42.2 58.7 %copy-start.1 = (bf16[2,2,56,512]{3,2,1,0:T(8,128)(2,1)}, bf16[2,2,56,512]{3,2,1,0:T(8,128)(2,1)S(1)}, u32[]{:S(2)}) copy-start(bf16[2,2,56,512]{3,2,1,0:T(8,128)(2,1)S(1)} %collective-permute-done.5.refs_1_.refs_6_) | copy-start | bytes 688132
  42.2 11.7 %collective-permute-start.23 = (f32[2,2,16,896]{3,2,1,0:T(8,128)}, f32[2,2,16,896]{3,2,1,0:T(8,128)S(1)}, u32[]{:S(2)}, u32[]{:S(2)}) collective-permute-start(f32[2,2,16,896]{3,2,1,0:T(8,128)} %get-tuple-element.46), channel_id=1, source_target_pairs={{0,3},{1,0},{2,1},{3,2},{4,7},{5,4},{6,5},{7,6},{8,11},{9,8},{10,9... | collective-permute-start | bytes 688136 | tf_op jit(solution)/shard_map/ppermute | solution.py:347
  43.5 57.4 %copy-start.9 = (bf16[2,56,512]{2,1,0:T(8,128)(2,1)}, bf16[2,56,512]{2,1,0:T(8,128)(2,1)S(1)}, u32[]{:S(2)}) copy-start(bf16[2,56,512]{2,1,0:T(8,128)(2,1)S(1)} %collective-permute-done.8.refs_9_) | copy-start | bytes 344068
  43.5 10.3 %collective-permute-start.11 = (bf16[2,2,56,512]{3,2,1,0:T(8,128)(2,1)S(1)}, bf16[2,2,56,512]{3,2,1,0:T(8,128)(2,1)S(1)}, u32[]{:S(2)}, u32[]{:S(2)}) collective-permute-start(bf16[2,2,56,512]{3,2,1,0:T(8,128)(2,1)S(1)} %gather.1), channel_id=1, source_target_pairs={{0,128},{8,136},{16,144},{24,152},{32,160},{40,168},{48,176},{56,1... | collective-permute-start | bytes 688136 | tf_op jit(solution)/shard_map/ppermute | solution.py:342
  46.9 7.6 %collective-permute-start.10 = (bf16[2,56,512]{2,1,0:T(8,128)(2,1)S(1)}, bf16[2,56,512]{2,1,0:T(8,128)(2,1)S(1)}, u32[]{:S(2)}, u32[]{:S(2)}) collective-permute-start(bf16[2,56,512]{2,1,0:T(8,128)(2,1)S(1)} %collective-permute-done.9.refs_10_), channel_id=1, source_target_pairs={{0,8},{8,0},{16,24},{24,16},{32,40},{40,32},{48,56},{56,48},{64,72... | collective-permute-start | bytes 344072 | tf_op jit(solution)/shard_map/ppermute | solution.py:342
  52.9 12.3 %collective-permute-start.4 = (bf16[2,2,56,512]{3,2,1,0:T(8,128)(2,1)S(1)}, bf16[2,2,56,512]{3,2,1,0:T(8,128)(2,1)S(1)}, u32[]{:S(2)}, u32[]{:S(2)}) collective-permute-start(bf16[2,2,56,512]{3,2,1,0:T(8,128)(2,1)S(1)} %collective-permute-done.3.refs_0_.refs_4_), channel_id=1, source_target_pairs={{0,8},{8,0},{16,24},{24,16},{32,40},{40,32},{48,56},{56,48},{64,72... | collective-permute-start | bytes 688136 | tf_op jit(solution)/shard_map/ppermute | solution.py:342
  53.8 14.5 %collective-permute-start.6 = (bf16[2,2,56,512]{3,2,1,0:T(8,128)(2,1)S(1)}, bf16[2,2,56,512]{3,2,1,0:T(8,128)(2,1)S(1)}, u32[]{:S(2)}, u32[]{:S(2)}) collective-permute-start(bf16[2,2,56,512]{3,2,1,0:T(8,128)(2,1)S(1)} %collective-permute-done.5.refs_1_.refs_6_), channel_id=1, source_target_pairs={{0,8},{8,0},{16,24},{24,16},{32,40},{40,32},{48,56},{56,48},{64,72... | collective-permute-start | bytes 688136 | tf_op jit(solution)/shard_map/ppermute | solution.py:342
  53.9 47.1 %copy-start.2 = (bf16[2,2,56,512]{3,2,1,0:T(8,128)(2,1)}, bf16[2,2,56,512]{3,2,1,0:T(8,128)(2,1)S(1)}, u32[]{:S(2)}) copy-start(bf16[2,2,56,512]{3,2,1,0:T(8,128)(2,1)S(1)} %collective-permute-done.11.refs_12_) | copy-start | bytes 688132
  53.9 14.5 %collective-permute-start.12 = (bf16[2,2,56,512]{3,2,1,0:T(8,128)(2,1)S(1)}, bf16[2,2,56,512]{3,2,1,0:T(8,128)(2,1)S(1)}, u32[]{:S(2)}, u32[]{:S(2)}) collective-permute-start(bf16[2,2,56,512]{3,2,1,0:T(8,128)(2,1)S(1)} %collective-permute-done.11.refs_12_), channel_id=1, source_target_pairs={{0,8},{8,0},{16,24},{24,16},{32,40},{40,32},{48,56},{56,48},{64,72... | collective-permute-start | bytes 688136 | tf_op jit(solution)/shard_map/ppermute | solution.py:342
  54.4 46.5 %copy-start.10 = (bf16[2,56,512]{2,1,0:T(8,128)(2,1)}, bf16[2,56,512]{2,1,0:T(8,128)(2,1)S(1)}, u32[]{:S(2)}) copy-start(bf16[2,56,512]{2,1,0:T(8,128)(2,1)S(1)} %collective-permute-done.10.refs_11_) | copy-start | bytes 344068
  54.4 6.2 %collective-permute-start.24 = (f32[2,16,896]{2,1,0:T(8,128)S(1)}, f32[2,16,896]{2,1,0:T(8,128)S(1)}, u32[]{:S(2)}, u32[]{:S(2)}) collective-permute-start(f32[2,16,896]{2,1,0:T(8,128)S(1)} %get-tuple-element.48), channel_id=1, source_target_pairs={{0,4},{1,5},{2,6},{3,7},{4,0},{5,1},{6,2},{7,3},{8,12},{9,13},{10,... | collective-permute-start | bytes 344072 | tf_op jit(solution)/shard_map/ppermute | solution.py:347
  57.0 43.9 %collective-permute-start.2 = (bf16[5,2,56,512]{3,2,1,0:T(8,128)(2,1)S(1)}, bf16[5,2,56,512]{3,2,1,0:T(8,128)(2,1)S(1)}, u32[]{:S(2)}, u32[]{:S(2)}) collective-permute-start(bf16[5,2,56,512]{3,2,1,0:T(8,128)(2,1)S(1)} %collective-permute-done.1.crossed.refs_2_), channel_id=1, source_target_pairs={{0,8},{8,0},{16,24},{24,16},{32,40},{40,32},{48,56},{56,48},{64,72... | collective-permute-start | bytes 1720328 | tf_op jit(solution)/shard_map/ppermute | solution.py:342
  60.6 17.9 %collective-permute-start.13 = (bf16[2,2,56,512]{3,2,1,0:T(8,128)(2,1)}, bf16[2,2,56,512]{3,2,1,0:T(8,128)(2,1)S(1)}, u32[]{:S(2)}, u32[]{:S(2)}) collective-permute-start(bf16[2,2,56,512]{3,2,1,0:T(8,128)(2,1)} %get-tuple-element.37), channel_id=1, source_target_pairs={{0,32},{8,40},{16,48},{24,56},{32,64},{40,72},{48,80},{56,88},{64,... | collective-permute-start | bytes 688136 | tf_op jit(solution)/shard_map/ppermute | solution.py:342
  65.2 35.8 %copy-start.3 = (bf16[2,2,56,512]{3,2,1,0:T(8,128)(2,1)}, bf16[2,2,56,512]{3,2,1,0:T(8,128)(2,1)S(1)}, u32[]{:S(2)}) copy-start(bf16[2,2,56,512]{3,2,1,0:T(8,128)(2,1)S(1)} %collective-permute-done.4.refs_5_) | copy-start | bytes 688132
  65.2 15.1 %collective-permute-start.15 = (bf16[2,2,56,512]{3,2,1,0:T(8,128)(2,1)}, bf16[2,2,56,512]{3,2,1,0:T(8,128)(2,1)S(1)}, u32[]{:S(2)}, u32[]{:S(2)}) collective-permute-start(bf16[2,2,56,512]{3,2,1,0:T(8,128)(2,1)} %get-tuple-element.38), channel_id=1, source_target_pairs={{0,96},{8,104},{16,112},{24,120},{32,0},{40,8},{48,16},{56,24},{64... | collective-permute-start | bytes 688136 | tf_op jit(solution)/shard_map/ppermute | solution.py:342
  68.3 32.6 %copy-start.4 = (bf16[2,2,56,512]{3,2,1,0:T(8,128)(2,1)}, bf16[2,2,56,512]{3,2,1,0:T(8,128)(2,1)S(1)}, u32[]{:S(2)}) copy-start(bf16[2,2,56,512]{3,2,1,0:T(8,128)(2,1)S(1)} %collective-permute-done.6.refs_7_) | copy-start | bytes 688132
  68.3 13.3 %collective-permute-start.17 = (bf16[2,2,56,512]{3,2,1,0:T(8,128)(2,1)}, bf16[2,2,56,512]{3,2,1,0:T(8,128)(2,1)S(1)}, u32[]{:S(2)}, u32[]{:S(2)}) collective-permute-start(bf16[2,2,56,512]{3,2,1,0:T(8,128)(2,1)} %get-tuple-element.39), channel_id=1, source_target_pairs={{0,16},{8,24},{16,32},{24,40},{32,48},{40,56},{48,64},{56,72},{64,... | collective-permute-start | bytes 688136 | tf_op jit(solution)/shard_map/ppermute | solution.py:342
  68.3 32.6 %copy-start.5 = (bf16[2,2,56,512]{3,2,1,0:T(8,128)(2,1)}, bf16[2,2,56,512]{3,2,1,0:T(8,128)(2,1)S(1)}, u32[]{:S(2)}) copy-start(bf16[2,2,56,512]{3,2,1,0:T(8,128)(2,1)S(1)} %collective-permute-done.12.refs_13_) | copy-start | bytes 688132
  68.4 15.3 %collective-permute-start.19 = (bf16[2,2,56,512]{3,2,1,0:T(8,128)(2,1)}, bf16[2,2,56,512]{3,2,1,0:T(8,128)(2,1)S(1)}, u32[]{:S(2)}, u32[]{:S(2)}) collective-permute-start(bf16[2,2,56,512]{3,2,1,0:T(8,128)(2,1)} %get-tuple-element.40), channel_id=1, source_target_pairs={{0,112},{8,120},{16,0},{24,8},{32,16},{40,24},{48,32},{56,40},{64,... | collective-permute-start | bytes 688136 | tf_op jit(solution)/shard_map/ppermute | solution.py:342
  78.5 22.3 %collective-permute-start.14 = (bf16[2,2,56,512]{3,2,1,0:T(8,128)(2,1)S(1)}, bf16[2,2,56,512]{3,2,1,0:T(8,128)(2,1)S(1)}, u32[]{:S(2)}, u32[]{:S(2)}) collective-permute-start(bf16[2,2,56,512]{3,2,1,0:T(8,128)(2,1)S(1)} %collective-permute-done.13.refs_14_), channel_id=1, source_target_pairs={{0,8},{8,0},{16,24},{24,16},{32,40},{40,32},{48,56},{56,48},{64,72... | collective-permute-start | bytes 688136 | tf_op jit(solution)/shard_map/ppermute | solution.py:342
  80.3 20.5 %collective-permute-start.16 = (bf16[2,2,56,512]{3,2,1,0:T(8,128)(2,1)S(1)}, bf16[2,2,56,512]{3,2,1,0:T(8,128)(2,1)S(1)}, u32[]{:S(2)}, u32[]{:S(2)}) collective-permute-start(bf16[2,2,56,512]{3,2,1,0:T(8,128)(2,1)S(1)} %collective-permute-done.15.refs_16_), channel_id=1, source_target_pairs={{0,8},{8,0},{16,24},{24,16},{32,40},{40,32},{48,56},{56,48},{64,72... | collective-permute-start | bytes 688136 | tf_op jit(solution)/shard_map/ppermute | solution.py:342
  81.6 19.2 %collective-permute-start.18 = (bf16[2,2,56,512]{3,2,1,0:T(8,128)(2,1)S(1)}, bf16[2,2,56,512]{3,2,1,0:T(8,128)(2,1)S(1)}, u32[]{:S(2)}, u32[]{:S(2)}) collective-permute-start(bf16[2,2,56,512]{3,2,1,0:T(8,128)(2,1)S(1)} %collective-permute-done.17.refs_18_), channel_id=1, source_target_pairs={{0,8},{8,0},{16,24},{24,16},{32,40},{40,32},{48,56},{56,48},{64,72... | collective-permute-start | bytes 688136 | tf_op jit(solution)/shard_map/ppermute | solution.py:342
  83.6 17.2 %collective-permute-start.20 = (bf16[2,2,56,512]{3,2,1,0:T(8,128)(2,1)S(1)}, bf16[2,2,56,512]{3,2,1,0:T(8,128)(2,1)S(1)}, u32[]{:S(2)}, u32[]{:S(2)}) collective-permute-start(bf16[2,2,56,512]{3,2,1,0:T(8,128)(2,1)S(1)} %collective-permute-done.19.refs_20_), channel_id=1, source_target_pairs={{0,8},{8,0},{16,24},{24,16},{32,40},{40,32},{48,56},{56,48},{64,72... | collective-permute-start | bytes 688136 | tf_op jit(solution)/shard_map/ppermute | solution.py:342
where the time goes:
time: 104 us
  starting transfers between devices  42.6 us (41%)
  waiting for transfers between devices  34.3 us (33%)
  blocking collectives  15.3 us (15%)
  Pallas kernels  10.9 us (10%)
    ppermute x21, starting transfers between devices, send(): return lax.ppermute(piece, ROW, hop(a, s, b))  35.1 us
    ppermute x21, waiting for transfers between devices, send(): return lax.ppermute(piece, ROW, hop(a, s, b))  23.7 us
    all_to_all x1, blocking collectives, body(): hid = lax.all_to_all(hid, ROW, 0, 0, tiled=True)  15.3 us
    ppermute x4, waiting for transfers between devices, side(): return lax.ppermute(piece, COL, pairs)  10.6 us
    ppermute x4, starting transfers between devices, side(): return lax.ppermute(piece, COL, pairs)  7.52 us
    pallas_call x1, Pallas kernels, pack_second(): pl.pallas_call(pack_second_kernel, out_shape=[hbm(2, *PIECE)] * 2 + [hbm(...  3.29 us
    pallas_call x1, Pallas kernels, unpack(): pl.pallas_call(unpack_kernel, out_shape=[hbm(2, 448, 512)] * 2, in_specs=...  2.99 us
    pallas_call x1, Pallas kernels, pack_first(): pl.pallas_call(pack_first_kernel, out_shape=[vmem(2, 2, *PIECE)] * 2 + [v...  2.2 us
  transfers between devices with their start and end apart: 25, of which 7 were waited for; matrix products, arithmetic and copies ran while one was open for 0% of the time, Pallas kernels for 2%

commit v1 on v0

--- a/solution.py
+++ b/solution.py
@@ -13,6 +13,8 @@
 LATE = (2, 6, 1, 7)
 FLIPPED = (0,) + LATE
 PIECES = tuple((a, s) for s in EARLY for a in (0, 1)) + ((0, 4), (1, 4)) + tuple((1, s) for s in FLIPPED) + tuple((0, s) for s in LATE) + ((0, 0),)
+FIRST = PIECES[:4] + PIECES[6:11]
+SECOND = PIECES[4:6] + PIECES[11:]
 PIECE = (56, 512)
 
 
@@ -54,7 +56,7 @@
     return pltpu.CompilerParams(vmem_limit_bytes=mib << 20)
 
 
-def selection(pieces, row_bits):
+def selection(pieces):
     x, z, c = lax.axis_index("xlo"), lax.axis_index("z"), lax.axis_index("core")
     row = lax.broadcasted_iota(jnp.int32, (16 * len(pieces), 256), 0)
     column = lax.broadcasted_iota(jnp.int32, (16 * len(pieces), 256), 1)
@@ -64,30 +66,30 @@
         flip = jnp.where(n == i, a, flip)
         step = jnp.where(n == i, s, step)
     block = ((flip ^ x) << 4) + (((z + step) & 7) << 1) + (b ^ c)
-    return (column == (j << row_bits) + block).astype(jnp.bfloat16)
+    return (column == (j << 5) + block).astype(jnp.bfloat16)
 
 
 def pack_first_kernel(w_hbm, *refs):
-    outs, w, sems = refs[:2], refs[2], refs[3]
+    outs, w, sems = refs[:3], refs[3], refs[4]
     copies = [pltpu.make_async_copy(w_hbm.at[pl.ds(8 * g, 8)], w.at[pl.ds(8 * g, 8)], sems.at[g]) for g in range(7)]
     for copy in copies:
         copy.start()
-    pick = selection(PIECES[:4], 5)
+    pick = selection(FIRST)
     for g in range(7):
         copies[g].wait()
         rows = w[8 * g : 8 * g + 8].reshape(256, 512)
         moved = jnp.dot(pick, rows, preferred_element_type=jnp.float32).astype(jnp.bfloat16)
-        moved = moved.reshape(2, 2, 2, 8, 512)
-        for i in range(2):
-            outs[i][:, :, 8 * g : 8 * g + 8, :] = moved[i]
+        moved = moved.reshape(9, 2, 8, 512)
+        for out, first, count in zip(outs, (0, 2, 4), (2, 2, 5)):
+            out[:, :, 8 * g : 8 * g + 8, :] = moved[first : first + count]
 
 
 def pack_first(w):
     return pl.pallas_call(
         pack_first_kernel,
-        out_shape=[vmem(2, 2, *PIECE)] * 2 + [vmem(56, 32, 512)],
+        out_shape=[vmem(2, 2, *PIECE)] * 2 + [vmem(5, 2, *PIECE), vmem(56, 32, 512)],
         in_specs=[INHBM],
-        out_specs=[WHOLE] * 3,
+        out_specs=[WHOLE] * 4,
         scratch_shapes=[pltpu.SemaphoreType.DMA((7,))],
         compiler_params=params(4),
         name="pack_first",
@@ -95,22 +97,21 @@
 
 
 def pack_second_kernel(w, probes_hbm, *refs):
-    outs, parts, (held, probes, proj, sems, out_sems, part_sems) = refs[:8], refs[8:12], refs[12:]
+    outs, parts, (held, probes, proj, sems, out_sems, part_sems) = refs[:7], refs[7:11], refs[11:]
     y = lax.axis_index("y")
     first = pltpu.make_async_copy(probes_hbm, probes, sems.at[0])
     first.start()
-    pick = selection(PIECES[4:], 5)
+    pick = selection(SECOND)
     dims = (((1,), (1,)), ((), ()))
     sent = []
 
     def ship(half, begin, count):
         rows = pl.ds(begin, count)
         pairs = [(held.at[i, :, rows], outs[i].at[:, rows]) for i in range(2)]
-        pairs.append((held.at[pl.ds(2, 5), :, rows], outs[2].at[:, :, rows]))
-        pairs += [(held.at[7 + i, :, rows], outs[3 + i].at[0, :, rows]) for i in range(4)]
-        pairs.append((held.at[11, :, rows], outs[7].at[:, rows]))
+        pairs += [(held.at[2 + i, :, rows], outs[2 + i].at[0, :, rows]) for i in range(4)]
+        pairs.append((held.at[6, :, rows], outs[6].at[:, rows]))
         for i, (source, target) in enumerate(pairs):
-            sent.append(pltpu.make_async_copy(source, target, out_sems.at[8 * half + i]))
+            sent.append(pltpu.make_async_copy(source, target, out_sems.at[7 * half + i]))
             sent[-1].start()
 
     for layer in range(2):
@@ -130,7 +131,7 @@
     for g in range(7):
         rows = w[8 * g : 8 * g + 8].reshape(256, 512)
         moved = jnp.dot(pick, rows, preferred_element_type=jnp.float32).astype(jnp.bfloat16)
-        held[:, :, 8 * g : 8 * g + 8, :] = moved.reshape(12, 2, 8, 512)
+        held[:, :, 8 * g : 8 * g + 8, :] = moved.reshape(7, 2, 8, 512)
         if g == 3:
             ship(0, 0, 32)
     ship(1, 32, 24)
@@ -142,19 +143,18 @@
     return pl.pallas_call(
         pack_second_kernel,
         out_shape=[hbm(2, *PIECE)] * 2
-        + [hbm(5, 2, *PIECE)]
         + [hbm(2, 2, *PIECE)] * 4
         + [hbm(2, *PIECE)]
         + [vmem(2, 2, 16, 896, dtype=jnp.float32)]
         + [hbm(2, 2, 16, 896, dtype=jnp.float32)] * 3,
         in_specs=[WHOLE, INHBM],
-        out_specs=[INHBM] * 8 + [WHOLE] + [INHBM] * 3,
+        out_specs=[INHBM] * 7 + [WHOLE] + [INHBM] * 3,
         scratch_shapes=[
-            pltpu.VMEM((12, 2, 56, 512), jnp.bfloat16),
+            pltpu.VMEM((7, 2, 56, 512), jnp.bfloat16),
             pltpu.VMEM((2, 128, 512), jnp.bfloat16),
             pltpu.VMEM((2, 8, 16, 896), jnp.float32),
             pltpu.SemaphoreType.DMA((1,)),
-            pltpu.SemaphoreType.DMA((16,)),
+            pltpu.SemaphoreType.DMA((14,)),
             pltpu.SemaphoreType.DMA((12,)),
         ],
         compiler_params=params(8),
@@ -163,10 +163,11 @@
 
 
 def join_kernel(crossed, *refs):
-    outs, sems = refs[4:8], refs[8]
+    outs, near, sems = refs[4:8], refs[8], refs[9]
     copies = [pltpu.make_async_copy(crossed.at[1 + n], out.at[1], sems.at[n]) for n, out in enumerate(outs)]
     for copy in copies:
         copy.start()
+    near[...] = crossed[0]
     for copy in copies:
         copy.wait()
 
@@ -174,9 +175,9 @@
 def join(crossed, straight):
     return pl.pallas_call(
         join_kernel,
-        out_shape=[hbm(2, 2, *PIECE)] * 4,
+        out_shape=[hbm(2, 2, *PIECE)] * 4 + [vmem(2, *PIECE)],
         in_specs=[WHOLE] + [INHBM] * 4,
-        out_specs=[INHBM] * 4,
+        out_specs=[INHBM] * 4 + [WHOLE],
         scratch_shapes=[pltpu.SemaphoreType.DMA((4,))],
         input_output_aliases={1: 0, 2: 1, 3: 2, 4: 3},
         compiler_params=params(1),
@@ -211,7 +212,7 @@
     local, crossed, z3, z5, d04, d14, post = early[0:2], early[2:4], early[4:6], early[6:8], early[8:10], early[10:12], early[12:14]
     pieces = []
     for b in range(2):
-        pieces += [(local[b].at[b], 0, 0, b), (crossed[b].at[0, b], 1, 0, b)]
+        pieces += [(local[b].at[b], 0, 0, b), (crossed[b].at[b], 1, 0, b)]
         pieces += [(z3[b].at[0, b], 0, 3, b), (post[b].at[0, b], 1, 3, b)]
         pieces += [(z5[b].at[0, b], 0, 5, b), (post[b].at[1, b], 1, 5, b)]
         pieces += [(d04[b].at[b], 0, 4, b), (d14[b].at[b], 1, 4, b)]
@@ -317,14 +318,14 @@
 
 def final_kernel(came, out_ref):
     turned = came[...].astype(jnp.float32).T.astype(jnp.bfloat16)
-    of = lax.broadcasted_iota(jnp.int32, (128, 448), 0)
-    to = lax.broadcasted_iota(jnp.int32, (128, 448), 1)
-    total = jnp.zeros((32, 448), jnp.float32)
-    for i in range(4):
-        unit = ((of & 3) << 2) + i
-        pick = ((to == (of >> 2) * 14 + unit) & (unit < 14)).astype(jnp.bfloat16)
-        total += jnp.dot(turned[32 * i : 32 * i + 32], pick, preferred_element_type=jnp.float32)
-    out_ref[...] = total.astype(jnp.bfloat16).reshape(2, 16, 448)
+    of = lax.broadcasted_iota(jnp.int32, (128, 512), 0)
+    to = lax.broadcasted_iota(jnp.int32, (128, 512), 1)
+    pick = (to == (of >> 2) * 14 + ((of & 3) << 2)).astype(jnp.bfloat16)
+    spread = jnp.dot(turned, pick, preferred_element_type=jnp.float32)
+    total = spread[:32]
+    for i in range(1, 4):
+        total += pltpu.roll(spread[32 * i : 32 * i + 32], i, 1)
+    out_ref[...] = total[:, :448].astype(jnp.bfloat16).reshape(2, 16, 448)
 
 
 def final(came):
@@ -351,18 +352,18 @@
     w = joined.reshape(2, 32, 28, 512).transpose(0, 2, 1, 3).reshape(56, 32, 512)
     *outs, w = pack_first(w)
     rest = pack_second(w, probes)
-    outs, parts = [*outs, *rest[:8]], rest[8:]
+    outs, parts = [*outs[:2], *rest[:2], outs[2], *rest[2:7]], rest[7:]
     early = [send(piece, 0, s, 0) for s, piece in zip(EARLY, outs)]
     across = [send(piece, a, 4, 0) for a, piece in zip((0, 1), outs[2:4])]
     crossed = send(outs[4], 1, 0, 0)
     parts = [parts[0]] + [side(parts[s], 0, s) for s in range(1, 4)]
     keep, give = halve(parts)
     came = side(give, 1, 0)
-    joins = join(crossed, outs[5:9])
+    *joins, near = join(crossed, outs[5:9])
     late = [send(piece, 0, s, 0) for s, piece in zip(LATE, joins)]
     post = gather(early)
     post = send(post, 1, 0, 0)
-    mine = early + across + [post, crossed] + late + [outs[9]]
+    mine = early + across + [post, near] + late + [outs[9]]
     other = [send(piece, 0, 0, 1) for piece in mine]
     hid = gated(keep, came).reshape(32, 4, 128)
     hid = lax.all_to_all(hid, ROW, 0, 0, tiled=True)

time: 104 us -> 95.4 us (0.917); the launches traced: 104 us -> 94 us
  waiting for transfers between devices: 34.3 us -> 15.3 us
  starting transfers between devices: 42.6 us -> 54.7 us
  blocking collectives: 15.3 us -> 12.1 us
    ppermute x21, starting transfers between devices: 35.1 us -> 47.2 us  [send(): return lax.ppermute(piece, ROW, hop(a, s, b))]
    ppermute x4, waiting for transfers between devices: 10.6 us -> 0.01 us  [side(): return lax.ppermute(piece, COL, pairs)]
    ppermute x21, waiting for transfers between devices: 23.7 us -> 15.3 us  [send(): return lax.ppermute(piece, ROW, hop(a, s, b))]
    all_to_all x1, blocking collectives: 15.3 us -> 12.1 us  [body(): hid = lax.all_to_all(hid, ROW, 0, 0, tiled=True)]
  transfers between devices with their start and end apart: 25 -> 25, of which waited for: 7 -> 4; matrix products, arithmetic and copies ran while one was open for 0% -> 0% of each run, Pallas kernels for 2% -> 6%
where the time goes in v1:
time: 95.4 us; the launch traced here: 94 us
  starting transfers between devices  54.7 us (57%)
  waiting for transfers between devices  15.3 us (16%)
  blocking collectives  12.1 us (13%)
  Pallas kernels  10.8 us (11%)
  between operations  1.02 us (1%)
    ppermute x21, starting transfers between devices, send(): return lax.ppermute(piece, ROW, hop(a, s, b))  47.2 us
    ppermute x21, waiting for transfers between devices, send(): return lax.ppermute(piece, ROW, hop(a, s, b))  15.3 us
    all_to_all x1, blocking collectives, body(): hid = lax.all_to_all(hid, ROW, 0, 0, tiled=True)  12.1 us
    ppermute x4, starting transfers between devices, side(): return lax.ppermute(piece, COL, pairs)  7.49 us
    pallas_call x1, Pallas kernels, pack_second(): pl.pallas_call(pack_second_kernel, out_shape=[hbm(2, *PIECE)] * 2 + [hbm(...  3.01 us
    pallas_call x1, Pallas kernels, unpack(): pl.pallas_call(unpack_kernel, out_shape=[hbm(2, 448, 512)] * 2, in_specs=...  2.98 us
    pallas_call x1, Pallas kernels, pack_first(): pl.pallas_call(pack_first_kernel, out_shape=[vmem(2, 2, *PIECE)] * 2 + [v...  2.37 us
  transfers between devices with their start and end apart: 25, of which 4 were waited for; matrix products, arithmetic and copies ran while one was open for 0% of the time, Pallas kernels for 6%

profile of v1, /device:TPU:1, one launch (start us, length us, event | category | flops | bytes accessed | tf_op | source)
XLA Modules:
  0.0 94.0 jit_solution(7227220116004851993)
XLA Ops:
  0.6 2.4 %pack_first.1 = (bf16[2,2,56,512]{3,2,1,0:T(8,128)(2,1)S(1)}, bf16[2,2,56,512]{3,2,1,0:T(8,128)(2,1)S(1)}, bf16[5,2,56,512]{3,2,1,0:T(8,128)(2,1)S(1)}, bf16[56,32,512]{2,1,0:T(8,128)(2,1)S(1)}) custom-call(bf16[56,32,512]{2,1,0:T(8,128)(2,1)} %bitcast.9), custom_call_target="tpu_custom_call" | custom-call | tf_op jit(solution)/shard_map/pack_first/pallas_call | solution.py:88
  3.0 2.1 %collective-permute-start.1 = (bf16[5,2,56,512]{3,2,1,0:T(8,128)(2,1)S(1)}, bf16[5,2,56,512]{3,2,1,0:T(8,128)(2,1)S(1)}, u32[]{:S(2)}, u32[]{:S(2)}) collective-permute-start(bf16[5,2,56,512]{3,2,1,0:T(8,128)(2,1)S(1)} %get-tuple-element.29), channel_id=1, source_target_pairs={{0,128},{8,136},{16,144},{24,152},{32,160},{40,168},{48,176},{56,1... | collective-permute-start | bytes 1720328 | tf_op jit(solution)/shard_map/ppermute | solution.py:343
  5.1 4.4 %collective-permute-start.3 = (bf16[2,2,56,512]{3,2,1,0:T(8,128)(2,1)S(1)}, bf16[2,2,56,512]{3,2,1,0:T(8,128)(2,1)S(1)}, u32[]{:S(2)}, u32[]{:S(2)}) collective-permute-start(bf16[2,2,56,512]{3,2,1,0:T(8,128)(2,1)S(1)} %get-tuple-element.35), channel_id=1, source_target_pairs={{0,48},{8,56},{16,64},{24,72},{32,80},{40,88},{48,96},{56,104},{64... | collective-permute-start | bytes 688136 | tf_op jit(solution)/shard_map/ppermute | solution.py:343
  9.5 3.0 %pack_second.1 = (bf16[2,56,512]{2,1,0:T(8,128)(2,1)}, bf16[2,56,512]{2,1,0:T(8,128)(2,1)}, bf16[2,2,56,512]{3,2,1,0:T(8,128)(2,1)}, bf16[2,2,56,512]{3,2,1,0:T(...) custom-call(bf16[56,32,512]{2,1,0:T(8,128)(2,1)S(1)} %get-tuple-elem, ...), custom_call_target="tpu_custom_call" | custom-call | tf_op jit(solution)/shard_map/pack_second/pallas_call | solution.py:143
  12.5 4.3 %collective-permute-start.7 = (bf16[2,56,512]{2,1,0:T(8,128)(2,1)}, bf16[2,56,512]{2,1,0:T(8,128)(2,1)S(1)}, u32[]{:S(2)}, u32[]{:S(2)}) collective-permute-start(bf16[2,56,512]{2,1,0:T(8,128)(2,1)} %get-tuple-element.37), channel_id=1, source_target_pairs={{0,64},{8,72},{16,80},{24,88},{32,96},{40,104},{48,112},{56,120},{... | collective-permute-start | bytes 344072 | tf_op jit(solution)/shard_map/ppermute | solution.py:343
  16.8 1.1 %collective-permute-start.9 = (bf16[2,56,512]{2,1,0:T(8,128)(2,1)}, bf16[2,56,512]{2,1,0:T(8,128)(2,1)S(1)}, u32[]{:S(2)}, u32[]{:S(2)}) collective-permute-start(bf16[2,56,512]{2,1,0:T(8,128)(2,1)} %get-tuple-element.38), channel_id=1, source_target_pairs={{0,192},{8,200},{16,208},{24,216},{32,224},{40,232},{48,240},{56,2... | collective-permute-start | bytes 344072 | tf_op jit(solution)/shard_map/ppermute | solution.py:343
  17.9 2.1 %collective-permute-start.5 = (bf16[2,2,56,512]{3,2,1,0:T(8,128)(2,1)S(1)}, bf16[2,2,56,512]{3,2,1,0:T(8,128)(2,1)S(1)}, u32[]{:S(2)}, u32[]{:S(2)}) collective-permute-start(bf16[2,2,56,512]{3,2,1,0:T(8,128)(2,1)S(1)} %get-tuple-element.36), channel_id=1, source_target_pairs={{0,80},{8,88},{16,96},{24,104},{32,112},{40,120},{48,0},{56,8},{64... | collective-permute-start | bytes 688136 | tf_op jit(solution)/shard_map/ppermute | solution.py:343
  20.1 8.1 %collective-permute-done.7.refs_8_ = bf16[2,56,512]{2,1,0:T(8,128)(2,1)S(1)} collective-permute-done((bf16[2,56,512]{2,1,0:T(8,128)(2,1)}, bf16[2,56,512]{2,1,0:T(8,128)(2,1)S(1)}, u32[]{:S(2)}, u32[]{:S(2)}) %collective-permute-start.7) | collective-permute-done | bytes 114720 | tf_op jit(solution)/shard_map/ppermute | solution.py:343
  28.2 1.3 %collective-permute-start.21 = (f32[2,2,16,896]{3,2,1,0:T(8,128)}, f32[2,2,16,896]{3,2,1,0:T(8,128)S(1)}, u32[]{:S(2)}, u32[]{:S(2)}) collective-permute-start(f32[2,2,16,896]{3,2,1,0:T(8,128)} %get-tuple-element.46), channel_id=1, source_target_pairs={{0,1},{1,2},{2,3},{3,0},{4,5},{5,6},{6,7},{7,4},{8,9},{9,10},{10,1... | collective-permute-start | bytes 688136 | tf_op jit(solution)/shard_map/ppermute | solution.py:348
  29.5 3.2 %collective-permute-done.9.refs_10_ = bf16[2,56,512]{2,1,0:T(8,128)(2,1)S(1)} collective-permute-done((bf16[2,56,512]{2,1,0:T(8,128)(2,1)}, bf16[2,56,512]{2,1,0:T(8,128)(2,1)S(1)}, u32[]{:S(2)}, u32[]{:S(2)}) %collective-permute-start.9) | collective-permute-done | bytes 114720 | tf_op jit(solution)/shard_map/ppermute | solution.py:343
  32.7 2.9 %collective-permute-start.22 = (f32[2,2,16,896]{3,2,1,0:T(8,128)}, f32[2,2,16,896]{3,2,1,0:T(8,128)S(1)}, u32[]{:S(2)}, u32[]{:S(2)}) collective-permute-start(f32[2,2,16,896]{3,2,1,0:T(8,128)} %get-tuple-element.47), channel_id=1, source_target_pairs={{0,2},{1,3},{2,0},{3,1},{4,6},{5,7},{6,4},{7,5},{8,10},{9,11},{10,... | collective-permute-start | bytes 688136 | tf_op jit(solution)/shard_map/ppermute | solution.py:348
  35.6 0.0 collective-permute-done.3.refs_0_.refs_4_
  35.6 0.8 collective-permute-start.23
  36.4 0.0 collective-permute-done.5.refs_1_.refs_6_
  36.4 4.1 %collective-permute-start = (bf16[2,56,512]{2,1,0:T(8,128)(2,1)}, bf16[2,56,512]{2,1,0:T(8,128)(2,1)S(1)}, u32[]{:S(2)}, u32[]{:S(2)}) collective-permute-start(bf16[2,56,512]{2,1,0:T(8,128)(2,1)} %get-tuple-element.28.refs_0_), channel_id=1, source_target_pairs={{0,8},{8,0},{16,24},{24,16},{32,40},{40,32},{48,56},{56,48},{64,72... | collective-permute-start | bytes 344072 | tf_op jit(solution)/shard_map/ppermute | solution.py:343
  40.5 0.0 collective-permute-done.21.p1
  40.5 1.9 %collective-permute-start.8 = (bf16[2,56,512]{2,1,0:T(8,128)(2,1)S(1)}, bf16[2,56,512]{2,1,0:T(8,128)(2,1)S(1)}, u32[]{:S(2)}, u32[]{:S(2)}) collective-permute-start(bf16[2,56,512]{2,1,0:T(8,128)(2,1)S(1)} %collective-permute-done.7.refs_8_), channel_id=1, source_target_pairs={{0,8},{8,0},{16,24},{24,16},{32,40},{40,32},{48,56},{56,48},{64,72... | collective-permute-start | bytes 344072 | tf_op jit(solution)/shard_map/ppermute | solution.py:343
  42.4 0.0 collective-permute-done.22.p2
  42.4 2.5 %collective-permute-start.4 = (bf16[2,2,56,512]{3,2,1,0:T(8,128)(2,1)S(1)}, bf16[2,2,56,512]{3,2,1,0:T(8,128)(2,1)S(1)}, u32[]{:S(2)}, u32[]{:S(2)}) collective-permute-start(bf16[2,2,56,512]{3,2,1,0:T(8,128)(2,1)S(1)} %collective-permute-done.3.refs_0_.refs_4_), channel_id=1, source_target_pairs={{0,8},{8,0},{16,24},{24,16},{32,40},{40,32},{48,56},{56,48},{64,72... | collective-permute-start | bytes 688136 | tf_op jit(solution)/shard_map/ppermute | solution.py:343
  44.9 0.3 gather.1
  45.2 1.3 %collective-permute-start.11 = (bf16[2,2,56,512]{3,2,1,0:T(8,128)(2,1)S(1)}, bf16[2,2,56,512]{3,2,1,0:T(8,128)(2,1)S(1)}, u32[]{:S(2)}, u32[]{:S(2)}) collective-permute-start(bf16[2,2,56,512]{3,2,1,0:T(8,128)(2,1)S(1)} %gather.1), channel_id=1, source_target_pairs={{0,128},{8,136},{16,144},{24,152},{32,160},{40,168},{48,176},{56,1... | collective-permute-start | bytes 688136 | tf_op jit(solution)/shard_map/ppermute | solution.py:343
  46.6 0.0 collective-permute-done.refs_1_
  46.6 2.8 %collective-permute-start.10 = (bf16[2,56,512]{2,1,0:T(8,128)(2,1)S(1)}, bf16[2,56,512]{2,1,0:T(8,128)(2,1)S(1)}, u32[]{:S(2)}, u32[]{:S(2)}) collective-permute-start(bf16[2,56,512]{2,1,0:T(8,128)(2,1)S(1)} %collective-permute-done.9.refs_10_), channel_id=1, source_target_pairs={{0,8},{8,0},{16,24},{24,16},{32,40},{40,32},{48,56},{56,48},{64,72... | collective-permute-start | bytes 344072 | tf_op jit(solution)/shard_map/ppermute | solution.py:343
  49.4 0.0 collective-permute-done.8.refs_9_
  49.4 2.5 %collective-permute-start.24 = (f32[2,16,896]{2,1,0:T(8,128)S(1)}, f32[2,16,896]{2,1,0:T(8,128)S(1)}, u32[]{:S(2)}, u32[]{:S(2)}) collective-permute-start(f32[2,16,896]{2,1,0:T(8,128)S(1)} %get-tuple-element.50), channel_id=1, source_target_pairs={{0,4},{1,5},{2,6},{3,7},{4,0},{5,1},{6,2},{7,3},{8,12},{9,13},{10,... | collective-permute-start | bytes 344072 | tf_op jit(solution)/shard_map/ppermute | solution.py:348
  51.9 0.0 collective-permute-done.1.crossed
  51.9 0.4 collective-permute-start.6
  52.3 0.8 join.1
  53.1 5.9 %collective-permute-start.13 = (bf16[2,2,56,512]{3,2,1,0:T(8,128)(2,1)}, bf16[2,2,56,512]{3,2,1,0:T(8,128)(2,1)S(1)}, u32[]{:S(2)}, u32[]{:S(2)}) collective-permute-start(bf16[2,2,56,512]{3,2,1,0:T(8,128)(2,1)} %get-tuple-element.39), channel_id=1, source_target_pairs={{0,32},{8,40},{16,48},{24,56},{32,64},{40,72},{48,80},{56,88},{64,... | collective-permute-start | bytes 688136 | tf_op jit(solution)/shard_map/ppermute | solution.py:343
  59.0 0.0 collective-permute-done.24.came
  59.0 5.0 %collective-permute-start.15 = (bf16[2,2,56,512]{3,2,1,0:T(8,128)(2,1)}, bf16[2,2,56,512]{3,2,1,0:T(8,128)(2,1)S(1)}, u32[]{:S(2)}, u32[]{:S(2)}) collective-permute-start(bf16[2,2,56,512]{3,2,1,0:T(8,128)(2,1)} %get-tuple-element.40), channel_id=1, source_target_pairs={{0,96},{8,104},{16,112},{24,120},{32,0},{40,8},{48,16},{56,24},{64... | collective-permute-start | bytes 688136 | tf_op jit(solution)/shard_map/ppermute | solution.py:343
  64.0 0.0 collective-permute-done.11.refs_12_
  64.0 2.7 %collective-permute-start.19 = (bf16[2,2,56,512]{3,2,1,0:T(8,128)(2,1)}, bf16[2,2,56,512]{3,2,1,0:T(8,128)(2,1)S(1)}, u32[]{:S(2)}, u32[]{:S(2)}) collective-permute-start(bf16[2,2,56,512]{3,2,1,0:T(8,128)(2,1)} %get-tuple-element.42), channel_id=1, source_target_pairs={{0,112},{8,120},{16,0},{24,8},{32,16},{40,24},{48,32},{56,40},{64,... | collective-permute-start | bytes 688136 | tf_op jit(solution)/shard_map/ppermute | solution.py:343
  66.7 0.0 collective-permute-done.6.refs_7_
  66.7 3.4 %collective-permute-start.12 = (bf16[2,2,56,512]{3,2,1,0:T(8,128)(2,1)S(1)}, bf16[2,2,56,512]{3,2,1,0:T(8,128)(2,1)S(1)}, u32[]{:S(2)}, u32[]{:S(2)}) collective-permute-start(bf16[2,2,56,512]{3,2,1,0:T(8,128)(2,1)S(1)} %collective-permute-done.11.refs_12_), channel_id=1, source_target_pairs={{0,8},{8,0},{16,24},{24,16},{32,40},{40,32},{48,56},{56,48},{64,72... | collective-permute-start | bytes 688136 | tf_op jit(solution)/shard_map/ppermute | solution.py:343
  70.1 0.0 collective-permute-done.13.refs_14_
  70.1 0.1 collective-permute-start.14
  70.2 1.7 %collective-permute-done.15.refs_16_ = bf16[2,2,56,512]{3,2,1,0:T(8,128)(2,1)S(1)} collective-permute-done((bf16[2,2,56,512]{3,2,1,0:T(8,128)(2,1)}, bf16[2,2,56,512]{3,2,1,0:T(8,128)(2,1)S(1)}, u32[]{:S(2)}, u32[]{:S(2)}) %collective-permute-start.15) | collective-permute-done | bytes 229408 | tf_op jit(solution)/shard_map/ppermute | solution.py:343
  71.9 0.9 collective-permute-start.16
  72.8 0.0 collective-permute-done.17.refs_18_
  72.8 1.5 %collective-permute-start.18 = (bf16[2,2,56,512]{3,2,1,0:T(8,128)(2,1)S(1)}, bf16[2,2,56,512]{3,2,1,0:T(8,128)(2,1)S(1)}, u32[]{:S(2)}, u32[]{:S(2)}) collective-permute-start(bf16[2,2,56,512]{3,2,1,0:T(8,128)(2,1)S(1)} %collective-permute-done.17.refs_18_), channel_id=1, source_target_pairs={{0,8},{8,0},{16,24},{24,16},{32,40},{40,32},{48,56},{56,48},{64,72... | collective-permute-start | bytes 688136 | tf_op jit(solution)/shard_map/ppermute | solution.py:343
  74.3 2.2 %collective-permute-done.19.refs_20_ = bf16[2,2,56,512]{3,2,1,0:T(8,128)(2,1)S(1)} collective-permute-done((bf16[2,2,56,512]{3,2,1,0:T(8,128)(2,1)}, bf16[2,2,56,512]{3,2,1,0:T(8,128)(2,1)S(1)}, u32[]{:S(2)}, u32[]{:S(2)}) %collective-permute-start.19) | collective-permute-done | bytes 229408 | tf_op jit(solution)/shard_map/ppermute | solution.py:343
  76.5 0.6 collective-permute-start.20
  77.2 0.1 collective-permute-start.2
  77.3 0.4 gated.1
  77.6 12.1 %all_to_all.5 = bf16[32,4,128]{2,1,0:T(4,128)(2,1)S(1)} all-to-all(bf16[32,4,128]{2,1,0:T(4,128)(2,1)S(1)} %bitcast.8), channel_id=1, replica_groups=mesh['xlo'=2,'z'=8,'core'=2,'xhi'=2,'y'=4] {'xlo','z','core'}, dimensions={0} | all-to-all | bytes 65536 | tf_op jit(solution)/shard_map/all_to_all | solution.py:369
  89.7 1.0 %final.1 = bf16[2,16,448]{2,1,0:T(8,128)(2,1)} custom-call(bf16[128,128]{1,0:T(8,128)(2,1)S(1)} %bitcast.7), custom_call_target="tpu_custom_call" | custom-call | tf_op jit(solution)/shard_map/final/pallas_call | solution.py:332
  90.8 3.0 %unpack.1 = (bf16[2,448,512]{2,1,0:T(8,128)(2,1)}, bf16[2,448,512]{2,1,0:T(8,128)(2,1)}) custom-call(bf16[2,56,512]{2,1,0:T(8,128)(2,1)} %get-tuple-element.28.refs_0_, bf16[2,56,512]{2,1,0:T(8,128)(2,1)} %copy-done.8, bf16[2,56,512]{2,1,0:T(8,128)(2,1)S(1)} %get-tuple-element.34.refs_2_, bf16[2,56,512]{2,1,0:T(8,128)(2,1)S(1)} %collective-permute-done.2.refs_3_, ...), custom_call_target="tpu_custom_call" | custom-call | tf_op jit(solution)/shard_map/unpack/pallas_call | solution.py:260
  (33 shorter events, 0.1 us)
Async XLA Ops:
  3.0 48.9 %collective-permute-start.1 = (bf16[5,2,56,512]{3,2,1,0:T(8,128)(2,1)S(1)}, bf16[5,2,56,512]{3,2,1,0:T(8,128)(2,1)S(1)}, u32[]{:S(2)}, u32[]{:S(2)}) collective-permute-start(bf16[5,2,56,512]{3,2,1,0:T(8,128)(2,1)S(1)} %get-tuple-element.29), channel_id=1, source_target_pairs={{0,128},{8,136},{16,144},{24,152},{32,160},{40,168},{48,176},{56,1... | collective-permute-start | bytes 1720328 | tf_op jit(solution)/shard_map/ppermute | solution.py:343
  5.1 30.5 %collective-permute-start.3 = (bf16[2,2,56,512]{3,2,1,0:T(8,128)(2,1)S(1)}, bf16[2,2,56,512]{3,2,1,0:T(8,128)(2,1)S(1)}, u32[]{:S(2)}, u32[]{:S(2)}) collective-permute-start(bf16[2,2,56,512]{3,2,1,0:T(8,128)(2,1)S(1)} %get-tuple-element.35), channel_id=1, source_target_pairs={{0,48},{8,56},{16,64},{24,72},{32,80},{40,88},{48,96},{56,104},{64... | collective-permute-start | bytes 688136 | tf_op jit(solution)/shard_map/ppermute | solution.py:343
  12.5 15.7 %collective-permute-start.7 = (bf16[2,56,512]{2,1,0:T(8,128)(2,1)}, bf16[2,56,512]{2,1,0:T(8,128)(2,1)S(1)}, u32[]{:S(2)}, u32[]{:S(2)}) collective-permute-start(bf16[2,56,512]{2,1,0:T(8,128)(2,1)} %get-tuple-element.37), channel_id=1, source_target_pairs={{0,64},{8,72},{16,80},{24,88},{32,96},{40,104},{48,112},{56,120},{... | collective-permute-start | bytes 344072 | tf_op jit(solution)/shard_map/ppermute | solution.py:343
  16.8 15.9 %collective-permute-start.9 = (bf16[2,56,512]{2,1,0:T(8,128)(2,1)}, bf16[2,56,512]{2,1,0:T(8,128)(2,1)S(1)}, u32[]{:S(2)}, u32[]{:S(2)}) collective-permute-start(bf16[2,56,512]{2,1,0:T(8,128)(2,1)} %get-tuple-element.38), channel_id=1, source_target_pairs={{0,192},{8,200},{16,208},{24,216},{32,224},{40,232},{48,240},{56,2... | collective-permute-start | bytes 344072 | tf_op jit(solution)/shard_map/ppermute | solution.py:343
  17.9 18.5 %collective-permute-start.5 = (bf16[2,2,56,512]{3,2,1,0:T(8,128)(2,1)S(1)}, bf16[2,2,56,512]{3,2,1,0:T(8,128)(2,1)S(1)}, u32[]{:S(2)}, u32[]{:S(2)}) collective-permute-start(bf16[2,2,56,512]{3,2,1,0:T(8,128)(2,1)S(1)} %get-tuple-element.36), channel_id=1, source_target_pairs={{0,80},{8,88},{16,96},{24,104},{32,112},{40,120},{48,0},{56,8},{64... | collective-permute-start | bytes 688136 | tf_op jit(solution)/shard_map/ppermute | solution.py:343
  28.2 62.5 %copy-start.6 = (bf16[2,56,512]{2,1,0:T(8,128)(2,1)}, bf16[2,56,512]{2,1,0:T(8,128)(2,1)S(1)}, u32[]{:S(2)}) copy-start(bf16[2,56,512]{2,1,0:T(8,128)(2,1)S(1)} %collective-permute-done.7.refs_8_) | copy-start | bytes 344068
  28.2 12.3 %collective-permute-start.21 = (f32[2,2,16,896]{3,2,1,0:T(8,128)}, f32[2,2,16,896]{3,2,1,0:T(8,128)S(1)}, u32[]{:S(2)}, u32[]{:S(2)}) collective-permute-start(f32[2,2,16,896]{3,2,1,0:T(8,128)} %get-tuple-element.46), channel_id=1, source_target_pairs={{0,1},{1,2},{2,3},{3,0},{4,5},{5,6},{6,7},{7,4},{8,9},{9,10},{10,1... | collective-permute-start | bytes 688136 | tf_op jit(solution)/shard_map/ppermute | solution.py:348
  32.7 58.0 %copy-start.7 = (bf16[2,56,512]{2,1,0:T(8,128)(2,1)}, bf16[2,56,512]{2,1,0:T(8,128)(2,1)S(1)}, u32[]{:S(2)}) copy-start(bf16[2,56,512]{2,1,0:T(8,128)(2,1)S(1)} %collective-permute-done.9.refs_10_) | copy-start | bytes 344068
  32.7 9.7 %collective-permute-start.22 = (f32[2,2,16,896]{3,2,1,0:T(8,128)}, f32[2,2,16,896]{3,2,1,0:T(8,128)S(1)}, u32[]{:S(2)}, u32[]{:S(2)}) collective-permute-start(f32[2,2,16,896]{3,2,1,0:T(8,128)} %get-tuple-element.47), channel_id=1, source_target_pairs={{0,2},{1,3},{2,0},{3,1},{4,6},{5,7},{6,4},{7,5},{8,10},{9,11},{10,... | collective-permute-start | bytes 688136 | tf_op jit(solution)/shard_map/ppermute | solution.py:348
  35.6 55.1 %copy-start = (bf16[2,2,56,512]{3,2,1,0:T(8,128)(2,1)}, bf16[2,2,56,512]{3,2,1,0:T(8,128)(2,1)S(1)}, u32[]{:S(2)}) copy-start(bf16[2,2,56,512]{3,2,1,0:T(8,128)(2,1)S(1)} %collective-permute-done.3.refs_0_.refs_4_) | copy-start | bytes 688132
  35.6 9.5 %collective-permute-start.23 = (f32[2,2,16,896]{3,2,1,0:T(8,128)}, f32[2,2,16,896]{3,2,1,0:T(8,128)S(1)}, u32[]{:S(2)}, u32[]{:S(2)}) collective-permute-start(f32[2,2,16,896]{3,2,1,0:T(8,128)} %get-tuple-element.48), channel_id=1, source_target_pairs={{0,3},{1,0},{2,1},{3,2},{4,7},{5,4},{6,5},{7,6},{8,11},{9,8},{10,9... | collective-permute-start | bytes 688136 | tf_op jit(solution)/shard_map/ppermute | solution.py:348
  36.4 54.3 %copy-start.1 = (bf16[2,2,56,512]{3,2,1,0:T(8,128)(2,1)}, bf16[2,2,56,512]{3,2,1,0:T(8,128)(2,1)S(1)}, u32[]{:S(2)}) copy-start(bf16[2,2,56,512]{3,2,1,0:T(8,128)(2,1)S(1)} %collective-permute-done.5.refs_1_.refs_6_) | copy-start | bytes 688132
  36.4 10.2 %collective-permute-start = (bf16[2,56,512]{2,1,0:T(8,128)(2,1)}, bf16[2,56,512]{2,1,0:T(8,128)(2,1)S(1)}, u32[]{:S(2)}, u32[]{:S(2)}) collective-permute-start(bf16[2,56,512]{2,1,0:T(8,128)(2,1)} %get-tuple-element.28.refs_0_), channel_id=1, source_target_pairs={{0,8},{8,0},{16,24},{24,16},{32,40},{40,32},{48,56},{56,48},{64,72... | collective-permute-start | bytes 344072 | tf_op jit(solution)/shard_map/ppermute | solution.py:343
  40.5 8.9 %collective-permute-start.8 = (bf16[2,56,512]{2,1,0:T(8,128)(2,1)S(1)}, bf16[2,56,512]{2,1,0:T(8,128)(2,1)S(1)}, u32[]{:S(2)}, u32[]{:S(2)}) collective-permute-start(bf16[2,56,512]{2,1,0:T(8,128)(2,1)S(1)} %collective-permute-done.7.refs_8_), channel_id=1, source_target_pairs={{0,8},{8,0},{16,24},{24,16},{32,40},{40,32},{48,56},{56,48},{64,72... | collective-permute-start | bytes 344072 | tf_op jit(solution)/shard_map/ppermute | solution.py:343
  42.4 21.6 %collective-permute-start.4 = (bf16[2,2,56,512]{3,2,1,0:T(8,128)(2,1)S(1)}, bf16[2,2,56,512]{3,2,1,0:T(8,128)(2,1)S(1)}, u32[]{:S(2)}, u32[]{:S(2)}) collective-permute-start(bf16[2,2,56,512]{3,2,1,0:T(8,128)(2,1)S(1)} %collective-permute-done.3.refs_0_.refs_4_), channel_id=1, source_target_pairs={{0,8},{8,0},{16,24},{24,16},{32,40},{40,32},{48,56},{56,48},{64,72... | collective-permute-start | bytes 688136 | tf_op jit(solution)/shard_map/ppermute | solution.py:343
  45.2 18.8 %collective-permute-start.11 = (bf16[2,2,56,512]{3,2,1,0:T(8,128)(2,1)S(1)}, bf16[2,2,56,512]{3,2,1,0:T(8,128)(2,1)S(1)}, u32[]{:S(2)}, u32[]{:S(2)}) collective-permute-start(bf16[2,2,56,512]{3,2,1,0:T(8,128)(2,1)S(1)} %gather.1), channel_id=1, source_target_pairs={{0,128},{8,136},{16,144},{24,152},{32,160},{40,168},{48,176},{56,1... | collective-permute-start | bytes 688136 | tf_op jit(solution)/shard_map/ppermute | solution.py:343
  46.6 44.2 %copy-start.8 = (bf16[2,56,512]{2,1,0:T(8,128)(2,1)}, bf16[2,56,512]{2,1,0:T(8,128)(2,1)S(1)}, u32[]{:S(2)}) copy-start(bf16[2,56,512]{2,1,0:T(8,128)(2,1)S(1)} %collective-permute-done.refs_1_) | copy-start | bytes 344068
  46.6 6.5 %collective-permute-start.10 = (bf16[2,56,512]{2,1,0:T(8,128)(2,1)S(1)}, bf16[2,56,512]{2,1,0:T(8,128)(2,1)S(1)}, u32[]{:S(2)}, u32[]{:S(2)}) collective-permute-start(bf16[2,56,512]{2,1,0:T(8,128)(2,1)S(1)} %collective-permute-done.9.refs_10_), channel_id=1, source_target_pairs={{0,8},{8,0},{16,24},{24,16},{32,40},{40,32},{48,56},{56,48},{64,72... | collective-permute-start | bytes 344072 | tf_op jit(solution)/shard_map/ppermute | solution.py:343
  49.4 41.3 %copy-start.9 = (bf16[2,56,512]{2,1,0:T(8,128)(2,1)}, bf16[2,56,512]{2,1,0:T(8,128)(2,1)S(1)}, u32[]{:S(2)}) copy-start(bf16[2,56,512]{2,1,0:T(8,128)(2,1)S(1)} %collective-permute-done.8.refs_9_) | copy-start | bytes 344068
  49.4 9.6 %collective-permute-start.24 = (f32[2,16,896]{2,1,0:T(8,128)S(1)}, f32[2,16,896]{2,1,0:T(8,128)S(1)}, u32[]{:S(2)}, u32[]{:S(2)}) collective-permute-start(f32[2,16,896]{2,1,0:T(8,128)S(1)} %get-tuple-element.50), channel_id=1, source_target_pairs={{0,4},{1,5},{2,6},{3,7},{4,0},{5,1},{6,2},{7,3},{8,12},{9,13},{10,... | collective-permute-start | bytes 344072 | tf_op jit(solution)/shard_map/ppermute | solution.py:348
  51.9 14.8 %collective-permute-start.6 = (bf16[2,2,56,512]{3,2,1,0:T(8,128)(2,1)S(1)}, bf16[2,2,56,512]{3,2,1,0:T(8,128)(2,1)S(1)}, u32[]{:S(2)}, u32[]{:S(2)}) collective-permute-start(bf16[2,2,56,512]{3,2,1,0:T(8,128)(2,1)S(1)} %collective-permute-done.5.refs_1_.refs_6_), channel_id=1, source_target_pairs={{0,8},{8,0},{16,24},{24,16},{32,40},{40,32},{48,56},{56,48},{64,72... | collective-permute-start | bytes 688136 | tf_op jit(solution)/shard_map/ppermute | solution.py:343
  53.1 37.6 %copy-start.10 = (bf16[2,56,512]{2,1,0:T(8,128)(2,1)}, bf16[2,56,512]{2,1,0:T(8,128)(2,1)S(1)}, u32[]{:S(2)}) copy-start(bf16[2,56,512]{2,1,0:T(8,128)(2,1)S(1)} %collective-permute-done.10.refs_11_) | copy-start | bytes 344068
  53.1 17.0 %collective-permute-start.13 = (bf16[2,2,56,512]{3,2,1,0:T(8,128)(2,1)}, bf16[2,2,56,512]{3,2,1,0:T(8,128)(2,1)S(1)}, u32[]{:S(2)}, u32[]{:S(2)}) collective-permute-start(bf16[2,2,56,512]{3,2,1,0:T(8,128)(2,1)} %get-tuple-element.39), channel_id=1, source_target_pairs={{0,32},{8,40},{16,48},{24,56},{32,64},{40,72},{48,80},{56,88},{64,... | collective-permute-start | bytes 688136 | tf_op jit(solution)/shard_map/ppermute | solution.py:343
  59.0 12.9 %collective-permute-start.15 = (bf16[2,2,56,512]{3,2,1,0:T(8,128)(2,1)}, bf16[2,2,56,512]{3,2,1,0:T(8,128)(2,1)S(1)}, u32[]{:S(2)}, u32[]{:S(2)}) collective-permute-start(bf16[2,2,56,512]{3,2,1,0:T(8,128)(2,1)} %get-tuple-element.40), channel_id=1, source_target_pairs={{0,96},{8,104},{16,112},{24,120},{32,0},{40,8},{48,16},{56,24},{64... | collective-permute-start | bytes 688136 | tf_op jit(solution)/shard_map/ppermute | solution.py:343
  64.0 26.8 %copy-start.2 = (bf16[2,2,56,512]{3,2,1,0:T(8,128)(2,1)}, bf16[2,2,56,512]{3,2,1,0:T(8,128)(2,1)S(1)}, u32[]{:S(2)}) copy-start(bf16[2,2,56,512]{3,2,1,0:T(8,128)(2,1)S(1)} %collective-permute-done.4.refs_5_) | copy-start | bytes 688132
  64.0 8.8 %collective-permute-start.17 = (bf16[2,2,56,512]{3,2,1,0:T(8,128)(2,1)}, bf16[2,2,56,512]{3,2,1,0:T(8,128)(2,1)S(1)}, u32[]{:S(2)}, u32[]{:S(2)}) collective-permute-start(bf16[2,2,56,512]{3,2,1,0:T(8,128)(2,1)} %get-tuple-element.41), channel_id=1, source_target_pairs={{0,16},{8,24},{16,32},{24,40},{32,48},{40,56},{48,64},{56,72},{64,... | collective-permute-start | bytes 688136 | tf_op jit(solution)/shard_map/ppermute | solution.py:343
  64.0 26.8 %copy-start.3 = (bf16[2,2,56,512]{3,2,1,0:T(8,128)(2,1)}, bf16[2,2,56,512]{3,2,1,0:T(8,128)(2,1)S(1)}, u32[]{:S(2)}) copy-start(bf16[2,2,56,512]{3,2,1,0:T(8,128)(2,1)S(1)} %collective-permute-done.11.refs_12_) | copy-start | bytes 688132
  64.0 12.5 %collective-permute-start.19 = (bf16[2,2,56,512]{3,2,1,0:T(8,128)(2,1)}, bf16[2,2,56,512]{3,2,1,0:T(8,128)(2,1)S(1)}, u32[]{:S(2)}, u32[]{:S(2)}) collective-permute-start(bf16[2,2,56,512]{3,2,1,0:T(8,128)(2,1)} %get-tuple-element.42), channel_id=1, source_target_pairs={{0,112},{8,120},{16,0},{24,8},{32,16},{40,24},{48,32},{56,40},{64,... | collective-permute-start | bytes 688136 | tf_op jit(solution)/shard_map/ppermute | solution.py:343
  66.7 24.1 %copy-start.4 = (bf16[2,2,56,512]{3,2,1,0:T(8,128)(2,1)}, bf16[2,2,56,512]{3,2,1,0:T(8,128)(2,1)S(1)}, u32[]{:S(2)}) copy-start(bf16[2,2,56,512]{3,2,1,0:T(8,128)(2,1)S(1)} %collective-permute-done.6.refs_7_) | copy-start | bytes 688132
  66.7 10.5 %collective-permute-start.12 = (bf16[2,2,56,512]{3,2,1,0:T(8,128)(2,1)S(1)}, bf16[2,2,56,512]{3,2,1,0:T(8,128)(2,1)S(1)}, u32[]{:S(2)}, u32[]{:S(2)}) collective-permute-start(bf16[2,2,56,512]{3,2,1,0:T(8,128)(2,1)S(1)} %collective-permute-done.11.refs_12_), channel_id=1, source_target_pairs={{0,8},{8,0},{16,24},{24,16},{32,40},{40,32},{48,56},{56,48},{64,72... | collective-permute-start | bytes 688136 | tf_op jit(solution)/shard_map/ppermute | solution.py:343
  70.1 20.5 %collective-permute-start.14 = (bf16[2,2,56,512]{3,2,1,0:T(8,128)(2,1)S(1)}, bf16[2,2,56,512]{3,2,1,0:T(8,128)(2,1)S(1)}, u32[]{:S(2)}, u32[]{:S(2)}) collective-permute-start(bf16[2,2,56,512]{3,2,1,0:T(8,128)(2,1)S(1)} %collective-permute-done.13.refs_14_), channel_id=1, source_target_pairs={{0,8},{8,0},{16,24},{24,16},{32,40},{40,32},{48,56},{56,48},{64,72... | collective-permute-start | bytes 688136 | tf_op jit(solution)/shard_map/ppermute | solution.py:343
  71.9 18.7 %collective-permute-start.16 = (bf16[2,2,56,512]{3,2,1,0:T(8,128)(2,1)S(1)}, bf16[2,2,56,512]{3,2,1,0:T(8,128)(2,1)S(1)}, u32[]{:S(2)}, u32[]{:S(2)}) collective-permute-start(bf16[2,2,56,512]{3,2,1,0:T(8,128)(2,1)S(1)} %collective-permute-done.15.refs_16_), channel_id=1, source_target_pairs={{0,8},{8,0},{16,24},{24,16},{32,40},{40,32},{48,56},{56,48},{64,72... | collective-permute-start | bytes 688136 | tf_op jit(solution)/shard_map/ppermute | solution.py:343
  72.8 17.9 %collective-permute-start.18 = (bf16[2,2,56,512]{3,2,1,0:T(8,128)(2,1)S(1)}, bf16[2,2,56,512]{3,2,1,0:T(8,128)(2,1)S(1)}, u32[]{:S(2)}, u32[]{:S(2)}) collective-permute-start(bf16[2,2,56,512]{3,2,1,0:T(8,128)(2,1)S(1)} %collective-permute-done.17.refs_18_), channel_id=1, source_target_pairs={{0,8},{8,0},{16,24},{24,16},{32,40},{40,32},{48,56},{56,48},{64,72... | collective-permute-start | bytes 688136 | tf_op jit(solution)/shard_map/ppermute | solution.py:343
  76.5 14.2 %collective-permute-start.20 = (bf16[2,2,56,512]{3,2,1,0:T(8,128)(2,1)S(1)}, bf16[2,2,56,512]{3,2,1,0:T(8,128)(2,1)S(1)}, u32[]{:S(2)}, u32[]{:S(2)}) collective-permute-start(bf16[2,2,56,512]{3,2,1,0:T(8,128)(2,1)S(1)} %collective-permute-done.19.refs_20_), channel_id=1, source_target_pairs={{0,8},{8,0},{16,24},{24,16},{32,40},{40,32},{48,56},{56,48},{64,72... | collective-permute-start | bytes 688136 | tf_op jit(solution)/shard_map/ppermute | solution.py:343
  77.2 13.6 %copy-start.5 = (bf16[2,2,56,512]{3,2,1,0:T(8,128)(2,1)}, bf16[2,2,56,512]{3,2,1,0:T(8,128)(2,1)S(1)}, u32[]{:S(2)}) copy-start(bf16[2,2,56,512]{3,2,1,0:T(8,128)(2,1)S(1)} %collective-permute-done.12.refs_13_) | copy-start | bytes 688132
  77.2 13.5 %collective-permute-start.2 = (bf16[2,56,512]{2,1,0:T(8,128)(2,1)S(1)}, bf16[2,56,512]{2,1,0:T(8,128)(2,1)S(1)}, u32[]{:S(2)}, u32[]{:S(2)}) collective-permute-start(bf16[2,56,512]{2,1,0:T(8,128)(2,1)S(1)} %get-tuple-element.34.refs_2_), channel_id=1, source_target_pairs={{0,8},{8,0},{16,24},{24,16},{32,40},{40,32},{48,56},{56,48},{64,72... | collective-permute-start | bytes 344072 | tf_op jit(solution)/shard_map/ppermute | solution.py:343

commit v2 on v1

--- a/solution.py
+++ b/solution.py
@@ -207,7 +207,7 @@
 
 
 def unpack_kernel(*refs):
-    early, late, (gate_hbm, up_hbm, held, rows_out, sems, out_sems) = refs[:14], refs[14:22], refs[22:]
+    early, late, (gate_hbm, up_hbm, held, rows_out, out_sems) = refs[:14], refs[14:22], refs[22:]
     x, z, c = lax.axis_index("xlo"), lax.axis_index("z"), lax.axis_index("core")
     local, crossed, z3, z5, d04, d14, post = early[0:2], early[2:4], early[4:6], early[6:8], early[8:10], early[10:12], early[12:14]
     pieces = []
@@ -220,10 +220,6 @@
     def place(a, s, b):
         return (a ^ x) * 4 + (((z - s) & 7) >> 1), (z - s) & 1, b ^ c
 
-    copies = []
-    for source, a, s, b in pieces:
-        copies.append(pltpu.make_async_copy(source, held.at[place(a, s, b)], sems.at[len(copies)]))
-        copies[-1].start()
     out = lax.broadcasted_iota(jnp.int32, (224, 224), 0)
     inn = lax.broadcasted_iota(jnp.int32, (224, 224), 1)
     source = jnp.zeros((224, 224), jnp.int32)
@@ -238,8 +234,8 @@
         for a in range(2):
             for b in range(2):
                 held[place(a, s, b)] = late[2 * i + b][a, b]
-    for copy in copies:
-        copy.wait()
+    for source, a, s, b in pieces:
+        held[place(a, s, b)] = source[...]
     copies = []
     for n in range(8):
         rows = held[n].reshape(224, 512)
@@ -260,17 +256,16 @@
     return pl.pallas_call(
         unpack_kernel,
         out_shape=[hbm(2, 448, 512)] * 2,
-        in_specs=[INHBM] * 2 + [ANYWHERE] * 2 + [INHBM] * 10 + [WHOLE] * 8,
+        in_specs=[WHOLE] * 22,
         out_specs=[INHBM] * 2,
         scratch_shapes=[
             pltpu.VMEM((8, 2, 2, 56, 512), jnp.bfloat16),
             pltpu.VMEM((8, 2, 2, 56, 512), jnp.bfloat16),
             pltpu.SemaphoreType.DMA((16,)),
-            pltpu.SemaphoreType.DMA((16,)),
         ],
         compiler_params=params(10),
         name="unpack",
-    )(*map(outside, early[:2]), *early[2:4], *map(outside, early[4:]), *map(inside, late))
+    )(*map(inside, early), *map(inside, late))
 
 
 def halve_kernel(p0, p1, p2, p3, keep, give):

time: 95.4 us -> 93.9 us (0.984)
  Pallas kernels: 10.8 us -> 9.58 us
    pallas_call x1, Pallas kernels: 2.98 us -> 1.72 us  [unpack(): pl.pallas_call(unpack_kernel, out_shape=[hbm(2, 448, 512)] * 2, in_specs=...]
where the time goes in v2:
time: 93.9 us; the launch traced here: 92.6 us
  starting transfers between devices  54.7 us (58%)
  waiting for transfers between devices  15.2 us (16%)
  blocking collectives  12.2 us (13%)
  Pallas kernels  9.58 us (10%)
    ppermute x21, starting transfers between devices, send(): return lax.ppermute(piece, ROW, hop(a, s, b))  47.2 us
    ppermute x21, waiting for transfers between devices, send(): return lax.ppermute(piece, ROW, hop(a, s, b))  15.2 us
    all_to_all x1, blocking collectives, body(): hid = lax.all_to_all(hid, ROW, 0, 0, tiled=True)  12.2 us
    ppermute x4, starting transfers between devices, side(): return lax.ppermute(piece, COL, pairs)  7.49 us
    pallas_call x1, Pallas kernels, pack_second(): pl.pallas_call(pack_second_kernel, out_shape=[hbm(2, *PIECE)] * 2 + [hbm(...  3.02 us
    pallas_call x1, Pallas kernels, pack_first(): pl.pallas_call(pack_first_kernel, out_shape=[vmem(2, 2, *PIECE)] * 2 + [v...  2.37 us
  transfers between devices with their start and end apart: 25, of which 4 were waited for; matrix products, arithmetic and copies ran while one was open for 0% of the time, Pallas kernels for 6%

profile of v2, /device:TPU:1, one launch (start us, length us, event | category | flops | bytes accessed | tf_op | source)
XLA Modules:
  0.0 92.6 jit_solution(7208034719572529380)
XLA Ops:
  0.6 2.4 %pack_first.1 = (bf16[2,2,56,512]{3,2,1,0:T(8,128)(2,1)S(1)}, bf16[2,2,56,512]{3,2,1,0:T(8,128)(2,1)S(1)}, bf16[5,2,56,512]{3,2,1,0:T(8,128)(2,1)S(1)}, bf16[56,32,512]{2,1,0:T(8,128)(2,1)S(1)}) custom-call(bf16[56,32,512]{2,1,0:T(8,128)(2,1)} %bitcast.9), custom_call_target="tpu_custom_call" | custom-call | tf_op jit(solution)/shard_map/pack_first/pallas_call | solution.py:88
  3.0 2.1 %collective-permute-start.1 = (bf16[5,2,56,512]{3,2,1,0:T(8,128)(2,1)S(1)}, bf16[5,2,56,512]{3,2,1,0:T(8,128)(2,1)S(1)}, u32[]{:S(2)}, u32[]{:S(2)}) collective-permute-start(bf16[5,2,56,512]{3,2,1,0:T(8,128)(2,1)S(1)} %get-tuple-element.29), channel_id=1, source_target_pairs={{0,128},{8,136},{16,144},{24,152},{32,160},{40,168},{48,176},{56,1... | collective-permute-start | bytes 1720328 | tf_op jit(solution)/shard_map/ppermute | solution.py:338
  5.1 4.4 %collective-permute-start.3 = (bf16[2,2,56,512]{3,2,1,0:T(8,128)(2,1)S(1)}, bf16[2,2,56,512]{3,2,1,0:T(8,128)(2,1)S(1)}, u32[]{:S(2)}, u32[]{:S(2)}) collective-permute-start(bf16[2,2,56,512]{3,2,1,0:T(8,128)(2,1)S(1)} %get-tuple-element.35), channel_id=1, source_target_pairs={{0,48},{8,56},{16,64},{24,72},{32,80},{40,88},{48,96},{56,104},{64... | collective-permute-start | bytes 688136 | tf_op jit(solution)/shard_map/ppermute | solution.py:338
  9.5 3.0 %pack_second.1 = (bf16[2,56,512]{2,1,0:T(8,128)(2,1)}, bf16[2,56,512]{2,1,0:T(8,128)(2,1)}, bf16[2,2,56,512]{3,2,1,0:T(8,128)(2,1)}, bf16[2,2,56,512]{3,2,1,0:T(...) custom-call(bf16[56,32,512]{2,1,0:T(8,128)(2,1)S(1)} %get-tuple-elem, ...), custom_call_target="tpu_custom_call" | custom-call | tf_op jit(solution)/shard_map/pack_second/pallas_call | solution.py:143
  12.5 4.3 %collective-permute-start.7 = (bf16[2,56,512]{2,1,0:T(8,128)(2,1)}, bf16[2,56,512]{2,1,0:T(8,128)(2,1)S(1)}, u32[]{:S(2)}, u32[]{:S(2)}) collective-permute-start(bf16[2,56,512]{2,1,0:T(8,128)(2,1)} %get-tuple-element.37), channel_id=1, source_target_pairs={{0,64},{8,72},{16,80},{24,88},{32,96},{40,104},{48,112},{56,120},{... | collective-permute-start | bytes 344072 | tf_op jit(solution)/shard_map/ppermute | solution.py:338
  16.8 1.1 %collective-permute-start.9 = (bf16[2,56,512]{2,1,0:T(8,128)(2,1)}, bf16[2,56,512]{2,1,0:T(8,128)(2,1)S(1)}, u32[]{:S(2)}, u32[]{:S(2)}) collective-permute-start(bf16[2,56,512]{2,1,0:T(8,128)(2,1)} %get-tuple-element.38), channel_id=1, source_target_pairs={{0,192},{8,200},{16,208},{24,216},{32,224},{40,232},{48,240},{56,2... | collective-permute-start | bytes 344072 | tf_op jit(solution)/shard_map/ppermute | solution.py:338
  17.9 2.1 %collective-permute-start.5 = (bf16[2,2,56,512]{3,2,1,0:T(8,128)(2,1)S(1)}, bf16[2,2,56,512]{3,2,1,0:T(8,128)(2,1)S(1)}, u32[]{:S(2)}, u32[]{:S(2)}) collective-permute-start(bf16[2,2,56,512]{3,2,1,0:T(8,128)(2,1)S(1)} %get-tuple-element.36), channel_id=1, source_target_pairs={{0,80},{8,88},{16,96},{24,104},{32,112},{40,120},{48,0},{56,8},{64... | collective-permute-start | bytes 688136 | tf_op jit(solution)/shard_map/ppermute | solution.py:338
  20.1 8.1 %collective-permute-done.7.refs_8_ = bf16[2,56,512]{2,1,0:T(8,128)(2,1)S(1)} collective-permute-done((bf16[2,56,512]{2,1,0:T(8,128)(2,1)}, bf16[2,56,512]{2,1,0:T(8,128)(2,1)S(1)}, u32[]{:S(2)}, u32[]{:S(2)}) %collective-permute-start.7) | collective-permute-done | bytes 114720 | tf_op jit(solution)/shard_map/ppermute | solution.py:338
  28.2 1.3 %collective-permute-start.21 = (f32[2,2,16,896]{3,2,1,0:T(8,128)}, f32[2,2,16,896]{3,2,1,0:T(8,128)S(1)}, u32[]{:S(2)}, u32[]{:S(2)}) collective-permute-start(f32[2,2,16,896]{3,2,1,0:T(8,128)} %get-tuple-element.46), channel_id=1, source_target_pairs={{0,1},{1,2},{2,3},{3,0},{4,5},{5,6},{6,7},{7,4},{8,9},{9,10},{10,1... | collective-permute-start | bytes 688136 | tf_op jit(solution)/shard_map/ppermute | solution.py:343
  29.5 3.2 %collective-permute-done.9.refs_10_ = bf16[2,56,512]{2,1,0:T(8,128)(2,1)S(1)} collective-permute-done((bf16[2,56,512]{2,1,0:T(8,128)(2,1)}, bf16[2,56,512]{2,1,0:T(8,128)(2,1)S(1)}, u32[]{:S(2)}, u32[]{:S(2)}) %collective-permute-start.9) | collective-permute-done | bytes 114720 | tf_op jit(solution)/shard_map/ppermute | solution.py:338
  32.7 2.9 %collective-permute-start.22 = (f32[2,2,16,896]{3,2,1,0:T(8,128)}, f32[2,2,16,896]{3,2,1,0:T(8,128)S(1)}, u32[]{:S(2)}, u32[]{:S(2)}) collective-permute-start(f32[2,2,16,896]{3,2,1,0:T(8,128)} %get-tuple-element.47), channel_id=1, source_target_pairs={{0,2},{1,3},{2,0},{3,1},{4,6},{5,7},{6,4},{7,5},{8,10},{9,11},{10,... | collective-permute-start | bytes 688136 | tf_op jit(solution)/shard_map/ppermute | solution.py:343
  35.6 0.8 collective-permute-start.23
  36.4 0.0 collective-permute-done.5.refs_1_.refs_6_
  36.4 4.1 %collective-permute-start = (bf16[2,56,512]{2,1,0:T(8,128)(2,1)}, bf16[2,56,512]{2,1,0:T(8,128)(2,1)S(1)}, u32[]{:S(2)}, u32[]{:S(2)}) collective-permute-start(bf16[2,56,512]{2,1,0:T(8,128)(2,1)} %get-tuple-element.28.refs_0_), channel_id=1, source_target_pairs={{0,8},{8,0},{16,24},{24,16},{32,40},{40,32},{48,56},{56,48},{64,72... | collective-permute-start | bytes 344072 | tf_op jit(solution)/shard_map/ppermute | solution.py:338
  40.5 0.0 collective-permute-done.21.p1
  40.5 2.0 %collective-permute-start.8 = (bf16[2,56,512]{2,1,0:T(8,128)(2,1)S(1)}, bf16[2,56,512]{2,1,0:T(8,128)(2,1)S(1)}, u32[]{:S(2)}, u32[]{:S(2)}) collective-permute-start(bf16[2,56,512]{2,1,0:T(8,128)(2,1)S(1)} %collective-permute-done.7.refs_8_), channel_id=1, source_target_pairs={{0,8},{8,0},{16,24},{24,16},{32,40},{40,32},{48,56},{56,48},{64,72... | collective-permute-start | bytes 344072 | tf_op jit(solution)/shard_map/ppermute | solution.py:338
  42.4 2.5 %collective-permute-start.4 = (bf16[2,2,56,512]{3,2,1,0:T(8,128)(2,1)S(1)}, bf16[2,2,56,512]{3,2,1,0:T(8,128)(2,1)S(1)}, u32[]{:S(2)}, u32[]{:S(2)}) collective-permute-start(bf16[2,2,56,512]{3,2,1,0:T(8,128)(2,1)S(1)} %collective-permute-done.3.refs_0_.refs_4_), channel_id=1, source_target_pairs={{0,8},{8,0},{16,24},{24,16},{32,40},{40,32},{48,56},{56,48},{64,72... | collective-permute-start | bytes 688136 | tf_op jit(solution)/shard_map/ppermute | solution.py:338
  44.9 0.3 gather.1
  45.2 0.0 collective-permute-done.23.p3
  45.2 1.3 %collective-permute-start.11 = (bf16[2,2,56,512]{3,2,1,0:T(8,128)(2,1)S(1)}, bf16[2,2,56,512]{3,2,1,0:T(8,128)(2,1)S(1)}, u32[]{:S(2)}, u32[]{:S(2)}) collective-permute-start(bf16[2,2,56,512]{3,2,1,0:T(8,128)(2,1)S(1)} %gather.1), channel_id=1, source_target_pairs={{0,128},{8,136},{16,144},{24,152},{32,160},{40,168},{48,176},{56,1... | collective-permute-start | bytes 688136 | tf_op jit(solution)/shard_map/ppermute | solution.py:338
  46.6 0.0 collective-permute-done.refs_1_
  46.6 2.8 %collective-permute-start.10 = (bf16[2,56,512]{2,1,0:T(8,128)(2,1)S(1)}, bf16[2,56,512]{2,1,0:T(8,128)(2,1)S(1)}, u32[]{:S(2)}, u32[]{:S(2)}) collective-permute-start(bf16[2,56,512]{2,1,0:T(8,128)(2,1)S(1)} %collective-permute-done.9.refs_10_), channel_id=1, source_target_pairs={{0,8},{8,0},{16,24},{24,16},{32,40},{40,32},{48,56},{56,48},{64,72... | collective-permute-start | bytes 344072 | tf_op jit(solution)/shard_map/ppermute | solution.py:338
  49.4 0.0 collective-permute-done.8.refs_9_
  49.4 2.5 %collective-permute-start.24 = (f32[2,16,896]{2,1,0:T(8,128)S(1)}, f32[2,16,896]{2,1,0:T(8,128)S(1)}, u32[]{:S(2)}, u32[]{:S(2)}) collective-permute-start(f32[2,16,896]{2,1,0:T(8,128)S(1)} %get-tuple-element.50), channel_id=1, source_target_pairs={{0,4},{1,5},{2,6},{3,7},{4,0},{5,1},{6,2},{7,3},{8,12},{9,13},{10,... | collective-permute-start | bytes 344072 | tf_op jit(solution)/shard_map/ppermute | solution.py:343
  51.9 0.4 collective-permute-start.6
  52.3 0.8 join.1
  53.1 5.9 %collective-permute-start.13 = (bf16[2,2,56,512]{3,2,1,0:T(8,128)(2,1)}, bf16[2,2,56,512]{3,2,1,0:T(8,128)(2,1)S(1)}, u32[]{:S(2)}, u32[]{:S(2)}) collective-permute-start(bf16[2,2,56,512]{3,2,1,0:T(8,128)(2,1)} %get-tuple-element.39), channel_id=1, source_target_pairs={{0,32},{8,40},{16,48},{24,56},{32,64},{40,72},{48,80},{56,88},{64,... | collective-permute-start | bytes 688136 | tf_op jit(solution)/shard_map/ppermute | solution.py:338
  59.0 0.0 collective-permute-done.24.came
  59.0 5.0 %collective-permute-start.15 = (bf16[2,2,56,512]{3,2,1,0:T(8,128)(2,1)}, bf16[2,2,56,512]{3,2,1,0:T(8,128)(2,1)S(1)}, u32[]{:S(2)}, u32[]{:S(2)}) collective-permute-start(bf16[2,2,56,512]{3,2,1,0:T(8,128)(2,1)} %get-tuple-element.40), channel_id=1, source_target_pairs={{0,96},{8,104},{16,112},{24,120},{32,0},{40,8},{48,16},{56,24},{64... | collective-permute-start | bytes 688136 | tf_op jit(solution)/shard_map/ppermute | solution.py:338
  64.0 0.0 collective-permute-done.4.refs_5_
  64.0 0.0 collective-permute-start.17
  64.0 0.0 collective-permute-done.11.refs_12_
  64.0 2.7 %collective-permute-start.19 = (bf16[2,2,56,512]{3,2,1,0:T(8,128)(2,1)}, bf16[2,2,56,512]{3,2,1,0:T(8,128)(2,1)S(1)}, u32[]{:S(2)}, u32[]{:S(2)}) collective-permute-start(bf16[2,2,56,512]{3,2,1,0:T(8,128)(2,1)} %get-tuple-element.42), channel_id=1, source_target_pairs={{0,112},{8,120},{16,0},{24,8},{32,16},{40,24},{48,32},{56,40},{64,... | collective-permute-start | bytes 688136 | tf_op jit(solution)/shard_map/ppermute | solution.py:338
  66.7 0.0 collective-permute-done.6.refs_7_
  66.7 3.4 %collective-permute-start.12 = (bf16[2,2,56,512]{3,2,1,0:T(8,128)(2,1)S(1)}, bf16[2,2,56,512]{3,2,1,0:T(8,128)(2,1)S(1)}, u32[]{:S(2)}, u32[]{:S(2)}) collective-permute-start(bf16[2,2,56,512]{3,2,1,0:T(8,128)(2,1)S(1)} %collective-permute-done.11.refs_12_), channel_id=1, source_target_pairs={{0,8},{8,0},{16,24},{24,16},{32,40},{40,32},{48,56},{56,48},{64,72... | collective-permute-start | bytes 688136 | tf_op jit(solution)/shard_map/ppermute | solution.py:338
  70.1 0.0 collective-permute-done.13.refs_14_
  70.1 0.1 collective-permute-start.14
  70.2 1.7 %collective-permute-done.15.refs_16_ = bf16[2,2,56,512]{3,2,1,0:T(8,128)(2,1)S(1)} collective-permute-done((bf16[2,2,56,512]{3,2,1,0:T(8,128)(2,1)}, bf16[2,2,56,512]{3,2,1,0:T(8,128)(2,1)S(1)}, u32[]{:S(2)}, u32[]{:S(2)}) %collective-permute-start.15) | collective-permute-done | bytes 229408 | tf_op jit(solution)/shard_map/ppermute | solution.py:338
  71.9 0.9 collective-permute-start.16
  72.8 1.5 %collective-permute-start.18 = (bf16[2,2,56,512]{3,2,1,0:T(8,128)(2,1)S(1)}, bf16[2,2,56,512]{3,2,1,0:T(8,128)(2,1)S(1)}, u32[]{:S(2)}, u32[]{:S(2)}) collective-permute-start(bf16[2,2,56,512]{3,2,1,0:T(8,128)(2,1)S(1)} %collective-permute-done.17.refs_18_), channel_id=1, source_target_pairs={{0,8},{8,0},{16,24},{24,16},{32,40},{40,32},{48,56},{56,48},{64,72... | collective-permute-start | bytes 688136 | tf_op jit(solution)/shard_map/ppermute | solution.py:338
  74.3 2.1 %collective-permute-done.19.refs_20_ = bf16[2,2,56,512]{3,2,1,0:T(8,128)(2,1)S(1)} collective-permute-done((bf16[2,2,56,512]{3,2,1,0:T(8,128)(2,1)}, bf16[2,2,56,512]{3,2,1,0:T(8,128)(2,1)S(1)}, u32[]{:S(2)}, u32[]{:S(2)}) %collective-permute-start.19) | collective-permute-done | bytes 229408 | tf_op jit(solution)/shard_map/ppermute | solution.py:338
  76.5 0.7 collective-permute-start.20
  77.1 0.0 collective-permute-start.2
  77.1 0.4 gated.1
  77.5 12.2 %all_to_all.5 = bf16[32,4,128]{2,1,0:T(4,128)(2,1)S(1)} all-to-all(bf16[32,4,128]{2,1,0:T(4,128)(2,1)S(1)} %bitcast.8), channel_id=1, replica_groups=mesh['xlo'=2,'z'=8,'core'=2,'xhi'=2,'y'=4] {'xlo','z','core'}, dimensions={0} | all-to-all | bytes 65536 | tf_op jit(solution)/shard_map/all_to_all | solution.py:364
  89.7 1.0 %final.1 = bf16[2,16,448]{2,1,0:T(8,128)(2,1)} custom-call(bf16[128,128]{1,0:T(8,128)(2,1)S(1)} %bitcast.7), custom_call_target="tpu_custom_call" | custom-call | tf_op jit(solution)/shard_map/final/pallas_call | solution.py:327
  90.7 0.0 collective-permute-done.2.refs_3_
  90.7 1.7 %unpack.1 = (bf16[2,448,512]{2,1,0:T(8,128)(2,1)}, bf16[2,448,512]{2,1,0:T(8,128)(2,1)}) custom-call(bf16[2,56,512]{2,1,0:T(8,128)(2,1)S(1)} %copy-done, bf16[2,56,512]{2,1,0:T(8,128)(2,1)S(1)} %collective-permute-done.refs_1_, bf16[2,56,512]{2,1,0:T(8,128)(2,1)S(1)} %get-tuple-element.34.refs_2_, bf16[2,56,512]{2,1,0:T(8,128)(2,1)S(1)} %collective-permute-done.2.refs_3_, ...), custom_call_target="tpu_custom_call" | custom-call | tf_op jit(solution)/shard_map/unpack/pallas_call | solution.py:256
  (13 shorter events, 0.1 us)
Async XLA Ops:
  3.0 48.9 %collective-permute-start.1 = (bf16[5,2,56,512]{3,2,1,0:T(8,128)(2,1)S(1)}, bf16[5,2,56,512]{3,2,1,0:T(8,128)(2,1)S(1)}, u32[]{:S(2)}, u32[]{:S(2)}) collective-permute-start(bf16[5,2,56,512]{3,2,1,0:T(8,128)(2,1)S(1)} %get-tuple-element.29), channel_id=1, source_target_pairs={{0,128},{8,136},{16,144},{24,152},{32,160},{40,168},{48,176},{56,1... | collective-permute-start | bytes 1720328 | tf_op jit(solution)/shard_map/ppermute | solution.py:338
  5.1 30.5 %collective-permute-start.3 = (bf16[2,2,56,512]{3,2,1,0:T(8,128)(2,1)S(1)}, bf16[2,2,56,512]{3,2,1,0:T(8,128)(2,1)S(1)}, u32[]{:S(2)}, u32[]{:S(2)}) collective-permute-start(bf16[2,2,56,512]{3,2,1,0:T(8,128)(2,1)S(1)} %get-tuple-element.35), channel_id=1, source_target_pairs={{0,48},{8,56},{16,64},{24,72},{32,80},{40,88},{48,96},{56,104},{64... | collective-permute-start | bytes 688136 | tf_op jit(solution)/shard_map/ppermute | solution.py:338
  12.5 78.2 %copy-start = (bf16[2,56,512]{2,1,0:T(8,128)(2,1)S(1)}, bf16[2,56,512]{2,1,0:T(8,128)(2,1)}, u32[]{:S(2)}) copy-start(bf16[2,56,512]{2,1,0:T(8,128)(2,1)} %get-tuple-element.28.refs_0_) | copy-start | bytes 344068
  12.5 15.6 %collective-permute-start.7 = (bf16[2,56,512]{2,1,0:T(8,128)(2,1)}, bf16[2,56,512]{2,1,0:T(8,128)(2,1)S(1)}, u32[]{:S(2)}, u32[]{:S(2)}) collective-permute-start(bf16[2,56,512]{2,1,0:T(8,128)(2,1)} %get-tuple-element.37), channel_id=1, source_target_pairs={{0,64},{8,72},{16,80},{24,88},{32,96},{40,104},{48,112},{56,120},{... | collective-permute-start | bytes 344072 | tf_op jit(solution)/shard_map/ppermute | solution.py:338
  16.8 15.9 %collective-permute-start.9 = (bf16[2,56,512]{2,1,0:T(8,128)(2,1)}, bf16[2,56,512]{2,1,0:T(8,128)(2,1)S(1)}, u32[]{:S(2)}, u32[]{:S(2)}) collective-permute-start(bf16[2,56,512]{2,1,0:T(8,128)(2,1)} %get-tuple-element.38), channel_id=1, source_target_pairs={{0,192},{8,200},{16,208},{24,216},{32,224},{40,232},{48,240},{56,2... | collective-permute-start | bytes 344072 | tf_op jit(solution)/shard_map/ppermute | solution.py:338
  17.9 18.5 %collective-permute-start.5 = (bf16[2,2,56,512]{3,2,1,0:T(8,128)(2,1)S(1)}, bf16[2,2,56,512]{3,2,1,0:T(8,128)(2,1)S(1)}, u32[]{:S(2)}, u32[]{:S(2)}) collective-permute-start(bf16[2,2,56,512]{3,2,1,0:T(8,128)(2,1)S(1)} %get-tuple-element.36), channel_id=1, source_target_pairs={{0,80},{8,88},{16,96},{24,104},{32,112},{40,120},{48,0},{56,8},{64... | collective-permute-start | bytes 688136 | tf_op jit(solution)/shard_map/ppermute | solution.py:338
  28.2 12.3 %collective-permute-start.21 = (f32[2,2,16,896]{3,2,1,0:T(8,128)}, f32[2,2,16,896]{3,2,1,0:T(8,128)S(1)}, u32[]{:S(2)}, u32[]{:S(2)}) collective-permute-start(f32[2,2,16,896]{3,2,1,0:T(8,128)} %get-tuple-element.46), channel_id=1, source_target_pairs={{0,1},{1,2},{2,3},{3,0},{4,5},{5,6},{6,7},{7,4},{8,9},{9,10},{10,1... | collective-permute-start | bytes 688136 | tf_op jit(solution)/shard_map/ppermute | solution.py:343
  32.7 9.7 %collective-permute-start.22 = (f32[2,2,16,896]{3,2,1,0:T(8,128)}, f32[2,2,16,896]{3,2,1,0:T(8,128)S(1)}, u32[]{:S(2)}, u32[]{:S(2)}) collective-permute-start(f32[2,2,16,896]{3,2,1,0:T(8,128)} %get-tuple-element.47), channel_id=1, source_target_pairs={{0,2},{1,3},{2,0},{3,1},{4,6},{5,7},{6,4},{7,5},{8,10},{9,11},{10,... | collective-permute-start | bytes 688136 | tf_op jit(solution)/shard_map/ppermute | solution.py:343
  35.6 9.5 %collective-permute-start.23 = (f32[2,2,16,896]{3,2,1,0:T(8,128)}, f32[2,2,16,896]{3,2,1,0:T(8,128)S(1)}, u32[]{:S(2)}, u32[]{:S(2)}) collective-permute-start(f32[2,2,16,896]{3,2,1,0:T(8,128)} %get-tuple-element.48), channel_id=1, source_target_pairs={{0,3},{1,0},{2,1},{3,2},{4,7},{5,4},{6,5},{7,6},{8,11},{9,8},{10,9... | collective-permute-start | bytes 688136 | tf_op jit(solution)/shard_map/ppermute | solution.py:343
  36.4 10.2 %collective-permute-start = (bf16[2,56,512]{2,1,0:T(8,128)(2,1)}, bf16[2,56,512]{2,1,0:T(8,128)(2,1)S(1)}, u32[]{:S(2)}, u32[]{:S(2)}) collective-permute-start(bf16[2,56,512]{2,1,0:T(8,128)(2,1)} %get-tuple-element.28.refs_0_), channel_id=1, source_target_pairs={{0,8},{8,0},{16,24},{24,16},{32,40},{40,32},{48,56},{56,48},{64,72... | collective-permute-start | bytes 344072 | tf_op jit(solution)/shard_map/ppermute | solution.py:338
  40.5 8.9 %collective-permute-start.8 = (bf16[2,56,512]{2,1,0:T(8,128)(2,1)S(1)}, bf16[2,56,512]{2,1,0:T(8,128)(2,1)S(1)}, u32[]{:S(2)}, u32[]{:S(2)}) collective-permute-start(bf16[2,56,512]{2,1,0:T(8,128)(2,1)S(1)} %collective-permute-done.7.refs_8_), channel_id=1, source_target_pairs={{0,8},{8,0},{16,24},{24,16},{32,40},{40,32},{48,56},{56,48},{64,72... | collective-permute-start | bytes 344072 | tf_op jit(solution)/shard_map/ppermute | solution.py:338
  42.4 21.6 %collective-permute-start.4 = (bf16[2,2,56,512]{3,2,1,0:T(8,128)(2,1)S(1)}, bf16[2,2,56,512]{3,2,1,0:T(8,128)(2,1)S(1)}, u32[]{:S(2)}, u32[]{:S(2)}) collective-permute-start(bf16[2,2,56,512]{3,2,1,0:T(8,128)(2,1)S(1)} %collective-permute-done.3.refs_0_.refs_4_), channel_id=1, source_target_pairs={{0,8},{8,0},{16,24},{24,16},{32,40},{40,32},{48,56},{56,48},{64,72... | collective-permute-start | bytes 688136 | tf_op jit(solution)/shard_map/ppermute | solution.py:338
  45.2 18.8 %collective-permute-start.11 = (bf16[2,2,56,512]{3,2,1,0:T(8,128)(2,1)S(1)}, bf16[2,2,56,512]{3,2,1,0:T(8,128)(2,1)S(1)}, u32[]{:S(2)}, u32[]{:S(2)}) collective-permute-start(bf16[2,2,56,512]{3,2,1,0:T(8,128)(2,1)S(1)} %gather.1), channel_id=1, source_target_pairs={{0,128},{8,136},{16,144},{24,152},{32,160},{40,168},{48,176},{56,1... | collective-permute-start | bytes 688136 | tf_op jit(solution)/shard_map/ppermute | solution.py:338
  46.6 6.5 %collective-permute-start.10 = (bf16[2,56,512]{2,1,0:T(8,128)(2,1)S(1)}, bf16[2,56,512]{2,1,0:T(8,128)(2,1)S(1)}, u32[]{:S(2)}, u32[]{:S(2)}) collective-permute-start(bf16[2,56,512]{2,1,0:T(8,128)(2,1)S(1)} %collective-permute-done.9.refs_10_), channel_id=1, source_target_pairs={{0,8},{8,0},{16,24},{24,16},{32,40},{40,32},{48,56},{56,48},{64,72... | collective-permute-start | bytes 344072 | tf_op jit(solution)/shard_map/ppermute | solution.py:338
  49.4 9.6 %collective-permute-start.24 = (f32[2,16,896]{2,1,0:T(8,128)S(1)}, f32[2,16,896]{2,1,0:T(8,128)S(1)}, u32[]{:S(2)}, u32[]{:S(2)}) collective-permute-start(f32[2,16,896]{2,1,0:T(8,128)S(1)} %get-tuple-element.50), channel_id=1, source_target_pairs={{0,4},{1,5},{2,6},{3,7},{4,0},{5,1},{6,2},{7,3},{8,12},{9,13},{10,... | collective-permute-start | bytes 344072 | tf_op jit(solution)/shard_map/ppermute | solution.py:343
  51.9 14.8 %collective-permute-start.6 = (bf16[2,2,56,512]{3,2,1,0:T(8,128)(2,1)S(1)}, bf16[2,2,56,512]{3,2,1,0:T(8,128)(2,1)S(1)}, u32[]{:S(2)}, u32[]{:S(2)}) collective-permute-start(bf16[2,2,56,512]{3,2,1,0:T(8,128)(2,1)S(1)} %collective-permute-done.5.refs_1_.refs_6_), channel_id=1, source_target_pairs={{0,8},{8,0},{16,24},{24,16},{32,40},{40,32},{48,56},{56,48},{64,72... | collective-permute-start | bytes 688136 | tf_op jit(solution)/shard_map/ppermute | solution.py:338
  53.1 17.0 %collective-permute-start.13 = (bf16[2,2,56,512]{3,2,1,0:T(8,128)(2,1)}, bf16[2,2,56,512]{3,2,1,0:T(8,128)(2,1)S(1)}, u32[]{:S(2)}, u32[]{:S(2)}) collective-permute-start(bf16[2,2,56,512]{3,2,1,0:T(8,128)(2,1)} %get-tuple-element.39), channel_id=1, source_target_pairs={{0,32},{8,40},{16,48},{24,56},{32,64},{40,72},{48,80},{56,88},{64,... | collective-permute-start | bytes 688136 | tf_op jit(solution)/shard_map/ppermute | solution.py:338
  59.0 13.0 %collective-permute-start.15 = (bf16[2,2,56,512]{3,2,1,0:T(8,128)(2,1)}, bf16[2,2,56,512]{3,2,1,0:T(8,128)(2,1)S(1)}, u32[]{:S(2)}, u32[]{:S(2)}) collective-permute-start(bf16[2,2,56,512]{3,2,1,0:T(8,128)(2,1)} %get-tuple-element.40), channel_id=1, source_target_pairs={{0,96},{8,104},{16,112},{24,120},{32,0},{40,8},{48,16},{56,24},{64... | collective-permute-start | bytes 688136 | tf_op jit(solution)/shard_map/ppermute | solution.py:338
  64.0 8.8 %collective-permute-start.17 = (bf16[2,2,56,512]{3,2,1,0:T(8,128)(2,1)}, bf16[2,2,56,512]{3,2,1,0:T(8,128)(2,1)S(1)}, u32[]{:S(2)}, u32[]{:S(2)}) collective-permute-start(bf16[2,2,56,512]{3,2,1,0:T(8,128)(2,1)} %get-tuple-element.41), channel_id=1, source_target_pairs={{0,16},{8,24},{16,32},{24,40},{32,48},{40,56},{48,64},{56,72},{64,... | collective-permute-start | bytes 688136 | tf_op jit(solution)/shard_map/ppermute | solution.py:338
  64.0 12.5 %collective-permute-start.19 = (bf16[2,2,56,512]{3,2,1,0:T(8,128)(2,1)}, bf16[2,2,56,512]{3,2,1,0:T(8,128)(2,1)S(1)}, u32[]{:S(2)}, u32[]{:S(2)}) collective-permute-start(bf16[2,2,56,512]{3,2,1,0:T(8,128)(2,1)} %get-tuple-element.42), channel_id=1, source_target_pairs={{0,112},{8,120},{16,0},{24,8},{32,16},{40,24},{48,32},{56,40},{64,... | collective-permute-start | bytes 688136 | tf_op jit(solution)/shard_map/ppermute | solution.py:338
  66.7 10.5 %collective-permute-start.12 = (bf16[2,2,56,512]{3,2,1,0:T(8,128)(2,1)S(1)}, bf16[2,2,56,512]{3,2,1,0:T(8,128)(2,1)S(1)}, u32[]{:S(2)}, u32[]{:S(2)}) collective-permute-start(bf16[2,2,56,512]{3,2,1,0:T(8,128)(2,1)S(1)} %collective-permute-done.11.refs_12_), channel_id=1, source_target_pairs={{0,8},{8,0},{16,24},{24,16},{32,40},{40,32},{48,56},{56,48},{64,72... | collective-permute-start | bytes 688136 | tf_op jit(solution)/shard_map/ppermute | solution.py:338
  70.1 20.6 %collective-permute-start.14 = (bf16[2,2,56,512]{3,2,1,0:T(8,128)(2,1)S(1)}, bf16[2,2,56,512]{3,2,1,0:T(8,128)(2,1)S(1)}, u32[]{:S(2)}, u32[]{:S(2)}) collective-permute-start(bf16[2,2,56,512]{3,2,1,0:T(8,128)(2,1)S(1)} %collective-permute-done.13.refs_14_), channel_id=1, source_target_pairs={{0,8},{8,0},{16,24},{24,16},{32,40},{40,32},{48,56},{56,48},{64,72... | collective-permute-start | bytes 688136 | tf_op jit(solution)/shard_map/ppermute | solution.py:338
  71.9 18.7 %collective-permute-start.16 = (bf16[2,2,56,512]{3,2,1,0:T(8,128)(2,1)S(1)}, bf16[2,2,56,512]{3,2,1,0:T(8,128)(2,1)S(1)}, u32[]{:S(2)}, u32[]{:S(2)}) collective-permute-start(bf16[2,2,56,512]{3,2,1,0:T(8,128)(2,1)S(1)} %collective-permute-done.15.refs_16_), channel_id=1, source_target_pairs={{0,8},{8,0},{16,24},{24,16},{32,40},{40,32},{48,56},{56,48},{64,72... | collective-permute-start | bytes 688136 | tf_op jit(solution)/shard_map/ppermute | solution.py:338
  72.8 17.9 %collective-permute-start.18 = (bf16[2,2,56,512]{3,2,1,0:T(8,128)(2,1)S(1)}, bf16[2,2,56,512]{3,2,1,0:T(8,128)(2,1)S(1)}, u32[]{:S(2)}, u32[]{:S(2)}) collective-permute-start(bf16[2,2,56,512]{3,2,1,0:T(8,128)(2,1)S(1)} %collective-permute-done.17.refs_18_), channel_id=1, source_target_pairs={{0,8},{8,0},{16,24},{24,16},{32,40},{40,32},{48,56},{56,48},{64,72... | collective-permute-start | bytes 688136 | tf_op jit(solution)/shard_map/ppermute | solution.py:338
  76.5 14.2 %collective-permute-start.20 = (bf16[2,2,56,512]{3,2,1,0:T(8,128)(2,1)S(1)}, bf16[2,2,56,512]{3,2,1,0:T(8,128)(2,1)S(1)}, u32[]{:S(2)}, u32[]{:S(2)}) collective-permute-start(bf16[2,2,56,512]{3,2,1,0:T(8,128)(2,1)S(1)} %collective-permute-done.19.refs_20_), channel_id=1, source_target_pairs={{0,8},{8,0},{16,24},{24,16},{32,40},{40,32},{48,56},{56,48},{64,72... | collective-permute-start | bytes 688136 | tf_op jit(solution)/shard_map/ppermute | solution.py:338
  77.1 13.5 %collective-permute-start.2 = (bf16[2,56,512]{2,1,0:T(8,128)(2,1)S(1)}, bf16[2,56,512]{2,1,0:T(8,128)(2,1)S(1)}, u32[]{:S(2)}, u32[]{:S(2)}) collective-permute-start(bf16[2,56,512]{2,1,0:T(8,128)(2,1)S(1)} %get-tuple-element.34.refs_2_), channel_id=1, source_target_pairs={{0,8},{8,0},{16,24},{24,16},{32,40},{40,32},{48,56},{56,48},{64,72... | collective-permute-start | bytes 344072 | tf_op jit(solution)/shard_map/ppermute | solution.py:338

commit v3 on v2

--- a/solution.py
+++ b/solution.py
@@ -97,7 +97,7 @@
 
 
 def pack_second_kernel(w, probes_hbm, *refs):
-    outs, parts, (held, probes, proj, sems, out_sems, part_sems) = refs[:7], refs[7:11], refs[11:]
+    outs, parts, (held, probes, proj, sems, out_sems, part_sems) = refs[:8], refs[8:12], refs[12:]
     y = lax.axis_index("y")
     first = pltpu.make_async_copy(probes_hbm, probes, sems.at[0])
     first.start()
@@ -108,10 +108,9 @@
     def ship(half, begin, count):
         rows = pl.ds(begin, count)
         pairs = [(held.at[i, :, rows], outs[i].at[:, rows]) for i in range(2)]
-        pairs += [(held.at[2 + i, :, rows], outs[2 + i].at[0, :, rows]) for i in range(4)]
-        pairs.append((held.at[6, :, rows], outs[6].at[:, rows]))
+        pairs.append((held.at[2, :, rows], outs[6].at[:, rows]))
         for i, (source, target) in enumerate(pairs):
-            sent.append(pltpu.make_async_copy(source, target, out_sems.at[7 * half + i]))
+            sent.append(pltpu.make_async_copy(source, target, out_sems.at[3 * half + i]))
             sent[-1].start()
 
     for layer in range(2):
@@ -131,7 +130,13 @@
     for g in range(7):
         rows = w[8 * g : 8 * g + 8].reshape(256, 512)
         moved = jnp.dot(pick, rows, preferred_element_type=jnp.float32).astype(jnp.bfloat16)
-        held[:, :, 8 * g : 8 * g + 8, :] = moved.reshape(7, 2, 8, 512)
+        moved = moved.reshape(7, 2, 8, 512)
+        here = slice(8 * g, 8 * g + 8)
+        held[:2, :, here, :] = moved[:2]
+        held[2, :, here, :] = moved[6]
+        for i in range(4):
+            outs[2 + i][0, 0, here, :] = moved[2 + i, 0]
+            outs[7][i, here, :] = moved[2 + i, 1]
         if g == 3:
             ship(0, 0, 32)
     ship(1, 32, 24)
@@ -143,18 +148,18 @@
     return pl.pallas_call(
         pack_second_kernel,
         out_shape=[hbm(2, *PIECE)] * 2
-        + [hbm(2, 2, *PIECE)] * 4
-        + [hbm(2, *PIECE)]
+        + [vmem(2, 2, *PIECE)] * 4
+        + [hbm(2, *PIECE), vmem(4, *PIECE)]
         + [vmem(2, 2, 16, 896, dtype=jnp.float32)]
         + [hbm(2, 2, 16, 896, dtype=jnp.float32)] * 3,
         in_specs=[WHOLE, INHBM],
-        out_specs=[INHBM] * 7 + [WHOLE] + [INHBM] * 3,
+        out_specs=[INHBM] * 2 + [WHOLE] * 4 + [INHBM] + [WHOLE] * 2 + [INHBM] * 3,
         scratch_shapes=[
-            pltpu.VMEM((7, 2, 56, 512), jnp.bfloat16),
+            pltpu.VMEM((3, 2, 56, 512), jnp.bfloat16),
             pltpu.VMEM((2, 128, 512), jnp.bfloat16),
             pltpu.VMEM((2, 8, 16, 896), jnp.float32),
             pltpu.SemaphoreType.DMA((1,)),
-            pltpu.SemaphoreType.DMA((14,)),
+            pltpu.SemaphoreType.DMA((6,)),
             pltpu.SemaphoreType.DMA((12,)),
         ],
         compiler_params=params(8),
@@ -162,27 +167,26 @@
     )(inside(w), outside(probes))
 
 
-def join_kernel(crossed, *refs):
-    outs, near, sems = refs[4:8], refs[8], refs[9]
-    copies = [pltpu.make_async_copy(crossed.at[1 + n], out.at[1], sems.at[n]) for n, out in enumerate(outs)]
-    for copy in copies:
-        copy.start()
-    near[...] = crossed[0]
-    for copy in copies:
-        copy.wait()
-
-
-def join(crossed, straight):
+def join_kernel(crossed, crossed_swapped, got, *refs):
+    outs, near = refs[4:8], refs[8]
+    for n, out in enumerate(outs):
+        out[0, 1] = got[n]
+        out[1, 0] = crossed[1 + n, 0]
+        out[1, 1] = crossed_swapped[1 + n, 1]
+    near[0] = crossed[0, 0]
+    near[1] = crossed_swapped[0, 1]
+
+
+def join(crossed, crossed_swapped, got, straight):
     return pl.pallas_call(
         join_kernel,
-        out_shape=[hbm(2, 2, *PIECE)] * 4 + [vmem(2, *PIECE)],
-        in_specs=[WHOLE] + [INHBM] * 4,
-        out_specs=[INHBM] * 4 + [WHOLE],
-        scratch_shapes=[pltpu.SemaphoreType.DMA((4,))],
-        input_output_aliases={1: 0, 2: 1, 3: 2, 4: 3},
+        out_shape=[vmem(2, 2, *PIECE)] * 4 + [vmem(2, *PIECE)],
+        in_specs=[WHOLE] * 7,
+        out_specs=[WHOLE] * 5,
+        input_output_aliases={3: 0, 4: 1, 5: 2, 6: 3},
         compiler_params=params(1),
         name="join",
-    )(inside(crossed), *map(outside, straight))
+    )(*map(inside, (crossed, crossed_swapped, got, *straight)))
 
 
 def gather_kernel(*refs):
@@ -207,12 +211,12 @@
 
 
 def unpack_kernel(*refs):
-    early, late, (gate_hbm, up_hbm, held, rows_out, out_sems) = refs[:14], refs[14:22], refs[22:]
+    early, late, (gate_hbm, up_hbm, held, rows_out, out_sems) = refs[:13], refs[13:17], refs[17:]
     x, z, c = lax.axis_index("xlo"), lax.axis_index("z"), lax.axis_index("core")
-    local, crossed, z3, z5, d04, d14, post = early[0:2], early[2:4], early[4:6], early[6:8], early[8:10], early[10:12], early[12:14]
+    local, near, z3, z5, d04, d14, post = early[0:2], early[2], early[3:5], early[5:7], early[7:9], early[9:11], early[11:13]
     pieces = []
     for b in range(2):
-        pieces += [(local[b].at[b], 0, 0, b), (crossed[b].at[b], 1, 0, b)]
+        pieces += [(local[b].at[b], 0, 0, b), (near.at[b], 1, 0, b)]
         pieces += [(z3[b].at[0, b], 0, 3, b), (post[b].at[0, b], 1, 3, b)]
         pieces += [(z5[b].at[0, b], 0, 5, b), (post[b].at[1, b], 1, 5, b)]
         pieces += [(d04[b].at[b], 0, 4, b), (d14[b].at[b], 1, 4, b)]
@@ -233,7 +237,7 @@
     for i, s in enumerate(LATE):
         for a in range(2):
             for b in range(2):
-                held[place(a, s, b)] = late[2 * i + b][a, b]
+                held[place(a, s, b)] = late[i][a, b]
     for source, a, s, b in pieces:
         held[place(a, s, b)] = source[...]
     copies = []
@@ -256,7 +260,7 @@
     return pl.pallas_call(
         unpack_kernel,
         out_shape=[hbm(2, 448, 512)] * 2,
-        in_specs=[WHOLE] * 22,
+        in_specs=[WHOLE] * 17,
         out_specs=[INHBM] * 2,
         scratch_shapes=[
             pltpu.VMEM((8, 2, 2, 56, 512), jnp.bfloat16),
@@ -347,24 +351,26 @@
     w = joined.reshape(2, 32, 28, 512).transpose(0, 2, 1, 3).reshape(56, 32, 512)
     *outs, w = pack_first(w)
     rest = pack_second(w, probes)
-    outs, parts = [*outs[:2], *rest[:2], outs[2], *rest[2:7]], rest[7:]
+    outs, give_core, parts = [*outs[:2], *rest[:2], outs[2], *rest[2:7]], rest[7], rest[8:]
     early = [send(piece, 0, s, 0) for s, piece in zip(EARLY, outs)]
     across = [send(piece, a, 4, 0) for a, piece in zip((0, 1), outs[2:4])]
     crossed = send(outs[4], 1, 0, 0)
     parts = [parts[0]] + [side(parts[s], 0, s) for s in range(1, 4)]
     keep, give = halve(parts)
     came = side(give, 1, 0)
-    *joins, near = join(crossed, outs[5:9])
+    got_core = send(give_core, 0, 0, 1)
+    crossed_swapped = send(crossed, 0, 0, 1)
+    *joins, near = join(crossed, crossed_swapped, got_core, outs[5:9])
     late = [send(piece, 0, s, 0) for s, piece in zip(LATE, joins)]
     post = gather(early)
     post = send(post, 1, 0, 0)
-    mine = early + across + [post, near] + late + [outs[9]]
+    mine = early + across + [post, outs[9]]
     other = [send(piece, 0, 0, 1) for piece in mine]
     hid = gated(keep, came).reshape(32, 4, 128)
     hid = lax.all_to_all(hid, ROW, 0, 0, tiled=True)
     hid = final(hid.reshape(128, 128))
     both = [piece for pair in zip(mine, other) for piece in pair]
-    gate_rows, up_rows = unpack(both[20:22] + both[10:12] + both[0:10], both[12:20])
+    gate_rows, up_rows = unpack(both[10:12] + [near] + both[:10], late)
     return gate_rows, up_rows, hid
 
 

time: 93.9 us -> 97.4 us (1.037); the launches traced: 92.6 us -> 97.3 us
  waiting for transfers between devices: 15.2 us -> 23.9 us
  starting transfers between devices: 54.7 us -> 48 us
  blocking collectives: 12.2 us -> 15.8 us
    ppermute x21 -> x18, starting transfers between devices: 47.2 us -> 40.2 us  [send(): return lax.ppermute(piece, ROW, hop(a, s, b))]
    ppermute x4, waiting for transfers between devices: 0.01 us -> 5.51 us  [side(): return lax.ppermute(piece, COL, pairs)]
    all_to_all x1, blocking collectives: 12.2 us -> 15.8 us  [body(): hid = lax.all_to_all(hid, ROW, 0, 0, tiled=True)]
    ppermute x21 -> x18, waiting for transfers between devices: 15.2 us -> 18.4 us  [send(): return lax.ppermute(piece, ROW, hop(a, s, b))]
  transfers between devices with their start and end apart: 25 -> 22, of which waited for: 4 -> 5; matrix products, arithmetic and copies ran while one was open for 0% -> 0% of each run, Pallas kernels for 6% -> 5%
where the time goes in v3:
time: 97.4 us; the launch traced here: 97.3 us
  starting transfers between devices  48 us (49%)
  waiting for transfers between devices  23.9 us (25%)
  blocking collectives  15.8 us (16%)
  Pallas kernels  8.63 us (9%)
    ppermute x18, starting transfers between devices, send(): return lax.ppermute(piece, ROW, hop(a, s, b))  40.2 us
    ppermute x18, waiting for transfers between devices, send(): return lax.ppermute(piece, ROW, hop(a, s, b))  18.4 us
    all_to_all x1, blocking collectives, body(): hid = lax.all_to_all(hid, ROW, 0, 0, tiled=True)  15.8 us
    ppermute x4, starting transfers between devices, side(): return lax.ppermute(piece, COL, pairs)  7.75 us
    ppermute x4, waiting for transfers between devices, side(): return lax.ppermute(piece, COL, pairs)  5.51 us
    pallas_call x1, Pallas kernels, pack_second(): pl.pallas_call(pack_second_kernel, out_shape=[hbm(2, *PIECE)] * 2 + [vmem...  2.8 us
    pallas_call x1, Pallas kernels, pack_first(): pl.pallas_call(pack_first_kernel, out_shape=[vmem(2, 2, *PIECE)] * 2 + [v...  2.37 us
  transfers between devices with their start and end apart: 22, of which 5 were waited for; matrix products, arithmetic and copies ran while one was open for 0% of the time, Pallas kernels for 5%

profile of v3, /device:TPU:1, one launch (start us, length us, event | category | flops | bytes accessed | tf_op | source)
XLA Modules:
  0.0 97.3 jit_solution(9518571364888656370)
XLA Ops:
  0.6 2.4 %pack_first.1 = (bf16[2,2,56,512]{3,2,1,0:T(8,128)(2,1)S(1)}, bf16[2,2,56,512]{3,2,1,0:T(8,128)(2,1)S(1)}, bf16[5,2,56,512]{3,2,1,0:T(8,128)(2,1)S(1)}, bf16[56,32,512]{2,1,0:T(8,128)(2,1)S(1)}) custom-call(bf16[56,32,512]{2,1,0:T(8,128)(2,1)} %bitcast.9), custom_call_target="tpu_custom_call" | custom-call | tf_op jit(solution)/shard_map/pack_first/pallas_call | solution.py:88
  3.0 2.1 %collective-permute-start.1 = (bf16[5,2,56,512]{3,2,1,0:T(8,128)(2,1)S(1)}, bf16[5,2,56,512]{3,2,1,0:T(8,128)(2,1)S(1)}, u32[]{:S(2)}, u32[]{:S(2)}) collective-permute-start(bf16[5,2,56,512]{3,2,1,0:T(8,128)(2,1)S(1)} %get-tuple-element.30), channel_id=1, source_target_pairs={{0,128},{8,136},{16,144},{24,152},{32,160},{40,168},{48,176},{56,1... | collective-permute-start | bytes 1720328 | tf_op jit(solution)/shard_map/ppermute | solution.py:342
  5.1 2.8 %pack_second.1 = (bf16[2,56,512]{2,1,0:T(8,128)(2,1)}, bf16[2,56,512]{2,1,0:T(8,128)(2,1)}, bf16[2,2,56,512]{3,2,1,0:T(8,128)(2,1)S(1)}, bf16[2,2,56,512]{3,2,1,...) custom-call(bf16[56,32,512]{2,1,0:T(8,128)(2,1)S(1)} %get-tuple-elem, ...), custom_call_target="tpu_custom_call" | custom-call | tf_op jit(solution)/shard_map/pack_second/pallas_call | solution.py:148
  7.9 7.0 %collective-permute-start.10 = (bf16[2,56,512]{2,1,0:T(8,128)(2,1)}, bf16[2,56,512]{2,1,0:T(8,128)(2,1)S(1)}, u32[]{:S(2)}, u32[]{:S(2)}) collective-permute-start(bf16[2,56,512]{2,1,0:T(8,128)(2,1)} %get-tuple-element.40), channel_id=1, source_target_pairs={{0,192},{8,200},{16,208},{24,216},{32,224},{40,232},{48,240},{56,2... | collective-permute-start | bytes 344072 | tf_op jit(solution)/shard_map/ppermute | solution.py:342
  14.9 4.1 %collective-permute-done.1.crossed = bf16[5,2,56,512]{3,2,1,0:T(8,128)(2,1)S(1)} collective-permute-done((bf16[5,2,56,512]{3,2,1,0:T(8,128)(2,1)S(1)}, bf16[5,2,56,512]{3,2,1,0:T(8,128)(2,1)S(1)}, u32[]{:S(2)}, u32[]{:S(2)}) %collective-permute-start.1) | collective-permute-done | bytes 573472 | tf_op jit(solution)/shard_map/ppermute | solution.py:342
  19.0 2.5 %collective-permute-start.2 = (bf16[5,2,56,512]{3,2,1,0:T(8,128)(2,1)S(1)}, bf16[5,2,56,512]{3,2,1,0:T(8,128)(2,1)S(1)}, u32[]{:S(2)}, u32[]{:S(2)}) collective-permute-start(bf16[5,2,56,512]{3,2,1,0:T(8,128)(2,1)S(1)} %collective-permute-done.1.crossed), channel_id=1, source_target_pairs={{0,8},{8,0},{16,24},{24,16},{32,40},{40,32},{48,56},{56,48},{64,72... | collective-permute-start | bytes 1720328 | tf_op jit(solution)/shard_map/ppermute | solution.py:342
  21.5 4.6 %collective-permute-start.4 = (bf16[2,2,56,512]{3,2,1,0:T(8,128)(2,1)S(1)}, bf16[2,2,56,512]{3,2,1,0:T(8,128)(2,1)S(1)}, u32[]{:S(2)}, u32[]{:S(2)}) collective-permute-start(bf16[2,2,56,512]{3,2,1,0:T(8,128)(2,1)S(1)} %get-tuple-element.37), channel_id=1, source_target_pairs={{0,48},{8,56},{16,64},{24,72},{32,80},{40,88},{48,96},{56,104},{64... | collective-permute-start | bytes 688136 | tf_op jit(solution)/shard_map/ppermute | solution.py:342
  26.1 2.1 %collective-permute-start.6 = (bf16[2,2,56,512]{3,2,1,0:T(8,128)(2,1)S(1)}, bf16[2,2,56,512]{3,2,1,0:T(8,128)(2,1)S(1)}, u32[]{:S(2)}, u32[]{:S(2)}) collective-permute-start(bf16[2,2,56,512]{3,2,1,0:T(8,128)(2,1)S(1)} %get-tuple-element.38), channel_id=1, source_target_pairs={{0,80},{8,88},{16,96},{24,104},{32,112},{40,120},{48,0},{56,8},{64... | collective-permute-start | bytes 688136 | tf_op jit(solution)/shard_map/ppermute | solution.py:342
  28.2 4.9 %collective-permute-start.8 = (bf16[2,56,512]{2,1,0:T(8,128)(2,1)}, bf16[2,56,512]{2,1,0:T(8,128)(2,1)S(1)}, u32[]{:S(2)}, u32[]{:S(2)}) collective-permute-start(bf16[2,56,512]{2,1,0:T(8,128)(2,1)} %get-tuple-element.39), channel_id=1, source_target_pairs={{0,64},{8,72},{16,80},{24,88},{32,96},{40,104},{48,112},{56,120},{... | collective-permute-start | bytes 344072 | tf_op jit(solution)/shard_map/ppermute | solution.py:342
  33.2 0.0 collective-permute-done.10.refs_9_
  33.2 0.8 collective-permute-start
  34.0 13.9 %collective-permute-done.8.refs_7_ = bf16[2,56,512]{2,1,0:T(8,128)(2,1)S(1)} collective-permute-done((bf16[2,56,512]{2,1,0:T(8,128)(2,1)}, bf16[2,56,512]{2,1,0:T(8,128)(2,1)S(1)}, u32[]{:S(2)}, u32[]{:S(2)}) %collective-permute-start.8) | collective-permute-done | bytes 114720 | tf_op jit(solution)/shard_map/ppermute | solution.py:342
  47.9 1.3 %collective-permute-start.18 = (f32[2,2,16,896]{3,2,1,0:T(8,128)}, f32[2,2,16,896]{3,2,1,0:T(8,128)S(1)}, u32[]{:S(2)}, u32[]{:S(2)}) collective-permute-start(f32[2,2,16,896]{3,2,1,0:T(8,128)} %get-tuple-element.48), channel_id=1, source_target_pairs={{0,1},{1,2},{2,3},{3,0},{4,5},{5,6},{6,7},{7,4},{8,9},{9,10},{10,1... | collective-permute-start | bytes 688136 | tf_op jit(solution)/shard_map/ppermute | solution.py:347
  49.2 0.0 collective-permute-done.refs_1_
  49.2 2.6 %collective-permute-start.19 = (f32[2,2,16,896]{3,2,1,0:T(8,128)}, f32[2,2,16,896]{3,2,1,0:T(8,128)S(1)}, u32[]{:S(2)}, u32[]{:S(2)}) collective-permute-start(f32[2,2,16,896]{3,2,1,0:T(8,128)} %get-tuple-element.49), channel_id=1, source_target_pairs={{0,2},{1,3},{2,0},{3,1},{4,6},{5,7},{6,4},{7,5},{8,10},{9,11},{10,... | collective-permute-start | bytes 688136 | tf_op jit(solution)/shard_map/ppermute | solution.py:347
  51.8 0.0 collective-permute-done.4.refs_0_.refs_3_
  51.8 1.1 %collective-permute-start.20 = (f32[2,2,16,896]{3,2,1,0:T(8,128)}, f32[2,2,16,896]{3,2,1,0:T(8,128)S(1)}, u32[]{:S(2)}, u32[]{:S(2)}) collective-permute-start(f32[2,2,16,896]{3,2,1,0:T(8,128)} %get-tuple-element.50), channel_id=1, source_target_pairs={{0,3},{1,0},{2,1},{3,2},{4,7},{5,4},{6,5},{7,6},{8,11},{9,8},{10,9... | collective-permute-start | bytes 688136 | tf_op jit(solution)/shard_map/ppermute | solution.py:347
  52.9 0.0 collective-permute-done.6.refs_1_.refs_5_
  52.9 1.8 %collective-permute-start.3 = (bf16[4,56,512]{2,1,0:T(8,128)(2,1)S(1)}, bf16[4,56,512]{2,1,0:T(8,128)(2,1)S(1)}, u32[]{:S(2)}, u32[]{:S(2)}) collective-permute-start(bf16[4,56,512]{2,1,0:T(8,128)(2,1)S(1)} %get-tuple-element.31), channel_id=1, source_target_pairs={{0,8},{8,0},{16,24},{24,16},{32,40},{40,32},{48,56},{56,48},{64,72... | collective-permute-start | bytes 688136 | tf_op jit(solution)/shard_map/ppermute | solution.py:342
  54.7 0.3 gather.1
  55.0 0.7 collective-permute-done.18.p1
  55.6 1.2 %collective-permute-start.12 = (bf16[2,2,56,512]{3,2,1,0:T(8,128)(2,1)S(1)}, bf16[2,2,56,512]{3,2,1,0:T(8,128)(2,1)S(1)}, u32[]{:S(2)}, u32[]{:S(2)}) collective-permute-start(bf16[2,2,56,512]{3,2,1,0:T(8,128)(2,1)S(1)} %gather.1), channel_id=1, source_target_pairs={{0,128},{8,136},{16,144},{24,152},{32,160},{40,168},{48,176},{56,1... | collective-permute-start | bytes 688136 | tf_op jit(solution)/shard_map/ppermute | solution.py:342
  56.8 4.9 %collective-permute-done.19.p2 = f32[2,2,16,896]{3,2,1,0:T(8,128)S(1)} collective-permute-done((f32[2,2,16,896]{3,2,1,0:T(8,128)}, f32[2,2,16,896]{3,2,1,0:T(8,128)S(1)}, u32[]{:S(2)}, u32[]{:S(2)}) %collective-permute-start.19) | collective-permute-done | bytes 229408 | tf_op jit(solution)/shard_map/ppermute | solution.py:347
  61.7 1.8 %collective-permute-start.11 = (bf16[2,56,512]{2,1,0:T(8,128)(2,1)S(1)}, bf16[2,56,512]{2,1,0:T(8,128)(2,1)S(1)}, u32[]{:S(2)}, u32[]{:S(2)}) collective-permute-start(bf16[2,56,512]{2,1,0:T(8,128)(2,1)S(1)} %collective-permute-done.10.refs_9_), channel_id=1, source_target_pairs={{0,8},{8,0},{16,24},{24,16},{32,40},{40,32},{48,56},{56,48},{64,72... | collective-permute-start | bytes 344072 | tf_op jit(solution)/shard_map/ppermute | solution.py:342
  63.5 0.0 collective-permute-done.20.p3
  63.5 0.0 collective-permute-start.5
  63.5 0.0 collective-permute-done.3.got
  63.5 0.5 collective-permute-start.7
  64.0 0.4 collective-permute-done.11.refs_10_
  64.4 0.4 collective-permute-start.9
  64.8 0.0 collective-permute-done.2.crossed_swapped
  64.8 2.8 %collective-permute-start.21 = (f32[2,16,896]{2,1,0:T(8,128)S(1)}, f32[2,16,896]{2,1,0:T(8,128)S(1)}, u32[]{:S(2)}, u32[]{:S(2)}) collective-permute-start(f32[2,16,896]{2,1,0:T(8,128)S(1)} %get-tuple-element.52), channel_id=1, source_target_pairs={{0,4},{1,5},{2,6},{3,7},{4,0},{5,1},{6,2},{7,3},{8,12},{9,13},{10,... | collective-permute-start | bytes 344072 | tf_op jit(solution)/shard_map/ppermute | solution.py:347
  67.6 0.1 join.1
  67.6 0.0 collective-permute-done.12.refs_11_
  67.6 0.7 collective-permute-start.13
  68.3 0.0 collective-permute-done.9.refs_8_
  68.3 2.8 %collective-permute-start.14 = (bf16[2,2,56,512]{3,2,1,0:T(8,128)(2,1)S(1)}, bf16[2,2,56,512]{3,2,1,0:T(8,128)(2,1)S(1)}, u32[]{:S(2)}, u32[]{:S(2)}) collective-permute-start(bf16[2,2,56,512]{3,2,1,0:T(8,128)(2,1)S(1)} %get-tuple-element.41), channel_id=1, source_target_pairs={{0,32},{8,40},{16,48},{24,56},{32,64},{40,72},{48,80},{56,88},{64,... | collective-permute-start | bytes 688136 | tf_op jit(solution)/shard_map/ppermute | solution.py:342
  71.1 4.0 %collective-permute-start.15 = (bf16[2,2,56,512]{3,2,1,0:T(8,128)(2,1)S(1)}, bf16[2,2,56,512]{3,2,1,0:T(8,128)(2,1)S(1)}, u32[]{:S(2)}, u32[]{:S(2)}) collective-permute-start(bf16[2,2,56,512]{3,2,1,0:T(8,128)(2,1)S(1)} %get-tuple-element.42), channel_id=1, source_target_pairs={{0,96},{8,104},{16,112},{24,120},{32,0},{40,8},{48,16},{56,24},{64... | collective-permute-start | bytes 688136 | tf_op jit(solution)/shard_map/ppermute | solution.py:342
  75.2 3.0 %collective-permute-start.16 = (bf16[2,2,56,512]{3,2,1,0:T(8,128)(2,1)S(1)}, bf16[2,2,56,512]{3,2,1,0:T(8,128)(2,1)S(1)}, u32[]{:S(2)}, u32[]{:S(2)}) collective-permute-start(bf16[2,2,56,512]{3,2,1,0:T(8,128)(2,1)S(1)} %get-tuple-element.43), channel_id=1, source_target_pairs={{0,16},{8,24},{16,32},{24,40},{32,48},{40,56},{48,64},{56,72},{64,... | collective-permute-start | bytes 688136 | tf_op jit(solution)/shard_map/ppermute | solution.py:342
  78.1 0.0 collective-permute-done.7.refs_6_
  78.1 0.0 collective-permute-start.17
  78.1 0.4 gated.1
  78.5 15.8 %all_to_all.5 = bf16[32,4,128]{2,1,0:T(4,128)(2,1)S(1)} all-to-all(bf16[32,4,128]{2,1,0:T(4,128)(2,1)S(1)} %bitcast.8), channel_id=1, replica_groups=mesh['xlo'=2,'z'=8,'core'=2,'xhi'=2,'y'=4] {'xlo','z','core'}, dimensions={0} | all-to-all | bytes 65536 | tf_op jit(solution)/shard_map/all_to_all | solution.py:370
  94.4 1.0 final.1
  95.3 0.0 collective-permute-done.13.refs_12_
  95.3 0.0 collective-permute-done.14.refs_13_
  95.3 0.0 collective-permute-done.16.refs_15_
  95.4 1.7 %unpack.1 = (bf16[2,448,512]{2,1,0:T(8,128)(2,1)}, bf16[2,448,512]{2,1,0:T(8,128)(2,1)}) custom-call(bf16[2,56,512]{2,1,0:T(8,128)(2,1)S(1)} %copy-done, bf16[2,56,512]{2,1,0:T(8,128)(2,1)S(1)} %collective-permute-done.refs_1_, bf16[2,56,512]{2,1,0:T(8,128)(2,1)S(1)} %get-tuple-element.36.refs_2_, ...), custom_call_target="tpu_custom_call" | custom-call | tf_op jit(solution)/shard_map/unpack/pallas_call | solution.py:260
  (7 shorter events, 0.1 us)
Async XLA Ops:
  3.0 16.0 %collective-permute-start.1 = (bf16[5,2,56,512]{3,2,1,0:T(8,128)(2,1)S(1)}, bf16[5,2,56,512]{3,2,1,0:T(8,128)(2,1)S(1)}, u32[]{:S(2)}, u32[]{:S(2)}) collective-permute-start(bf16[5,2,56,512]{3,2,1,0:T(8,128)(2,1)S(1)} %get-tuple-element.30), channel_id=1, source_target_pairs={{0,128},{8,136},{16,144},{24,152},{32,160},{40,168},{48,176},{56,1... | collective-permute-start | bytes 1720328 | tf_op jit(solution)/shard_map/ppermute | solution.py:342
  7.9 25.2 %collective-permute-start.10 = (bf16[2,56,512]{2,1,0:T(8,128)(2,1)}, bf16[2,56,512]{2,1,0:T(8,128)(2,1)S(1)}, u32[]{:S(2)}, u32[]{:S(2)}) collective-permute-start(bf16[2,56,512]{2,1,0:T(8,128)(2,1)} %get-tuple-element.40), channel_id=1, source_target_pairs={{0,192},{8,200},{16,208},{24,216},{32,224},{40,232},{48,240},{56,2... | collective-permute-start | bytes 344072 | tf_op jit(solution)/shard_map/ppermute | solution.py:342
  19.0 45.8 %collective-permute-start.2 = (bf16[5,2,56,512]{3,2,1,0:T(8,128)(2,1)S(1)}, bf16[5,2,56,512]{3,2,1,0:T(8,128)(2,1)S(1)}, u32[]{:S(2)}, u32[]{:S(2)}) collective-permute-start(bf16[5,2,56,512]{3,2,1,0:T(8,128)(2,1)S(1)} %collective-permute-done.1.crossed), channel_id=1, source_target_pairs={{0,8},{8,0},{16,24},{24,16},{32,40},{40,32},{48,56},{56,48},{64,72... | collective-permute-start | bytes 1720328 | tf_op jit(solution)/shard_map/ppermute | solution.py:342
  21.5 30.3 %collective-permute-start.4 = (bf16[2,2,56,512]{3,2,1,0:T(8,128)(2,1)S(1)}, bf16[2,2,56,512]{3,2,1,0:T(8,128)(2,1)S(1)}, u32[]{:S(2)}, u32[]{:S(2)}) collective-permute-start(bf16[2,2,56,512]{3,2,1,0:T(8,128)(2,1)S(1)} %get-tuple-element.37), channel_id=1, source_target_pairs={{0,48},{8,56},{16,64},{24,72},{32,80},{40,88},{48,96},{56,104},{64... | collective-permute-start | bytes 688136 | tf_op jit(solution)/shard_map/ppermute | solution.py:342
  26.1 26.8 %collective-permute-start.6 = (bf16[2,2,56,512]{3,2,1,0:T(8,128)(2,1)S(1)}, bf16[2,2,56,512]{3,2,1,0:T(8,128)(2,1)S(1)}, u32[]{:S(2)}, u32[]{:S(2)}) collective-permute-start(bf16[2,2,56,512]{3,2,1,0:T(8,128)(2,1)S(1)} %get-tuple-element.38), channel_id=1, source_target_pairs={{0,80},{8,88},{16,96},{24,104},{32,112},{40,120},{48,0},{56,8},{64... | collective-permute-start | bytes 688136 | tf_op jit(solution)/shard_map/ppermute | solution.py:342
  28.2 19.6 %collective-permute-start.8 = (bf16[2,56,512]{2,1,0:T(8,128)(2,1)}, bf16[2,56,512]{2,1,0:T(8,128)(2,1)S(1)}, u32[]{:S(2)}, u32[]{:S(2)}) collective-permute-start(bf16[2,56,512]{2,1,0:T(8,128)(2,1)} %get-tuple-element.39), channel_id=1, source_target_pairs={{0,64},{8,72},{16,80},{24,88},{32,96},{40,104},{48,112},{56,120},{... | collective-permute-start | bytes 344072 | tf_op jit(solution)/shard_map/ppermute | solution.py:342
  33.2 16.0 %collective-permute-start = (bf16[2,56,512]{2,1,0:T(8,128)(2,1)}, bf16[2,56,512]{2,1,0:T(8,128)(2,1)S(1)}, u32[]{:S(2)}, u32[]{:S(2)}) collective-permute-start(bf16[2,56,512]{2,1,0:T(8,128)(2,1)} %get-tuple-element.29.refs_0_), channel_id=1, source_target_pairs={{0,8},{8,0},{16,24},{24,16},{32,40},{40,32},{48,56},{56,48},{64,72... | collective-permute-start | bytes 344072 | tf_op jit(solution)/shard_map/ppermute | solution.py:342
  47.9 7.8 %collective-permute-start.18 = (f32[2,2,16,896]{3,2,1,0:T(8,128)}, f32[2,2,16,896]{3,2,1,0:T(8,128)S(1)}, u32[]{:S(2)}, u32[]{:S(2)}) collective-permute-start(f32[2,2,16,896]{3,2,1,0:T(8,128)} %get-tuple-element.48), channel_id=1, source_target_pairs={{0,1},{1,2},{2,3},{3,0},{4,5},{5,6},{6,7},{7,4},{8,9},{9,10},{10,1... | collective-permute-start | bytes 688136 | tf_op jit(solution)/shard_map/ppermute | solution.py:347
  49.2 12.5 %collective-permute-start.19 = (f32[2,2,16,896]{3,2,1,0:T(8,128)}, f32[2,2,16,896]{3,2,1,0:T(8,128)S(1)}, u32[]{:S(2)}, u32[]{:S(2)}) collective-permute-start(f32[2,2,16,896]{3,2,1,0:T(8,128)} %get-tuple-element.49), channel_id=1, source_target_pairs={{0,2},{1,3},{2,0},{3,1},{4,6},{5,7},{6,4},{7,5},{8,10},{9,11},{10,... | collective-permute-start | bytes 688136 | tf_op jit(solution)/shard_map/ppermute | solution.py:347
  51.8 11.7 %collective-permute-start.20 = (f32[2,2,16,896]{3,2,1,0:T(8,128)}, f32[2,2,16,896]{3,2,1,0:T(8,128)S(1)}, u32[]{:S(2)}, u32[]{:S(2)}) collective-permute-start(f32[2,2,16,896]{3,2,1,0:T(8,128)} %get-tuple-element.50), channel_id=1, source_target_pairs={{0,3},{1,0},{2,1},{3,2},{4,7},{5,4},{6,5},{7,6},{8,11},{9,8},{10,9... | collective-permute-start | bytes 688136 | tf_op jit(solution)/shard_map/ppermute | solution.py:347
  52.9 10.6 %collective-permute-start.3 = (bf16[4,56,512]{2,1,0:T(8,128)(2,1)S(1)}, bf16[4,56,512]{2,1,0:T(8,128)(2,1)S(1)}, u32[]{:S(2)}, u32[]{:S(2)}) collective-permute-start(bf16[4,56,512]{2,1,0:T(8,128)(2,1)S(1)} %get-tuple-element.31), channel_id=1, source_target_pairs={{0,8},{8,0},{16,24},{24,16},{32,40},{40,32},{48,56},{56,48},{64,72... | collective-permute-start | bytes 688136 | tf_op jit(solution)/shard_map/ppermute | solution.py:342
  55.0 40.4 %copy-start = (bf16[2,56,512]{2,1,0:T(8,128)(2,1)S(1)}, bf16[2,56,512]{2,1,0:T(8,128)(2,1)}, u32[]{:S(2)}) copy-start(bf16[2,56,512]{2,1,0:T(8,128)(2,1)} %get-tuple-element.29.refs_0_) | copy-start | bytes 344068
  55.6 12.0 %collective-permute-start.12 = (bf16[2,2,56,512]{3,2,1,0:T(8,128)(2,1)S(1)}, bf16[2,2,56,512]{3,2,1,0:T(8,128)(2,1)S(1)}, u32[]{:S(2)}, u32[]{:S(2)}) collective-permute-start(bf16[2,2,56,512]{3,2,1,0:T(8,128)(2,1)S(1)} %gather.1), channel_id=1, source_target_pairs={{0,128},{8,136},{16,144},{24,152},{32,160},{40,168},{48,176},{56,1... | collective-permute-start | bytes 688136 | tf_op jit(solution)/shard_map/ppermute | solution.py:342
  61.7 2.8 %collective-permute-start.11 = (bf16[2,56,512]{2,1,0:T(8,128)(2,1)S(1)}, bf16[2,56,512]{2,1,0:T(8,128)(2,1)S(1)}, u32[]{:S(2)}, u32[]{:S(2)}) collective-permute-start(bf16[2,56,512]{2,1,0:T(8,128)(2,1)S(1)} %collective-permute-done.10.refs_9_), channel_id=1, source_target_pairs={{0,8},{8,0},{16,24},{24,16},{32,40},{40,32},{48,56},{56,48},{64,72... | collective-permute-start | bytes 344072 | tf_op jit(solution)/shard_map/ppermute | solution.py:342
  63.5 11.7 %collective-permute-start.5 = (bf16[2,2,56,512]{3,2,1,0:T(8,128)(2,1)S(1)}, bf16[2,2,56,512]{3,2,1,0:T(8,128)(2,1)S(1)}, u32[]{:S(2)}, u32[]{:S(2)}) collective-permute-start(bf16[2,2,56,512]{3,2,1,0:T(8,128)(2,1)S(1)} %collective-permute-done.4.refs_0_.refs_3_), channel_id=1, source_target_pairs={{0,8},{8,0},{16,24},{24,16},{32,40},{40,32},{48,56},{56,48},{64,72... | collective-permute-start | bytes 688136 | tf_op jit(solution)/shard_map/ppermute | solution.py:342
  63.5 14.7 %collective-permute-start.7 = (bf16[2,2,56,512]{3,2,1,0:T(8,128)(2,1)S(1)}, bf16[2,2,56,512]{3,2,1,0:T(8,128)(2,1)S(1)}, u32[]{:S(2)}, u32[]{:S(2)}) collective-permute-start(bf16[2,2,56,512]{3,2,1,0:T(8,128)(2,1)S(1)} %collective-permute-done.6.refs_1_.refs_5_), channel_id=1, source_target_pairs={{0,8},{8,0},{16,24},{24,16},{32,40},{40,32},{48,56},{56,48},{64,72... | collective-permute-start | bytes 688136 | tf_op jit(solution)/shard_map/ppermute | solution.py:342
  64.4 3.9 %collective-permute-start.9 = (bf16[2,56,512]{2,1,0:T(8,128)(2,1)S(1)}, bf16[2,56,512]{2,1,0:T(8,128)(2,1)S(1)}, u32[]{:S(2)}, u32[]{:S(2)}) collective-permute-start(bf16[2,56,512]{2,1,0:T(8,128)(2,1)S(1)} %collective-permute-done.8.refs_7_), channel_id=1, source_target_pairs={{0,8},{8,0},{16,24},{24,16},{32,40},{40,32},{48,56},{56,48},{64,72... | collective-permute-start | bytes 344072 | tf_op jit(solution)/shard_map/ppermute | solution.py:342
  64.8 6.3 %collective-permute-start.21 = (f32[2,16,896]{2,1,0:T(8,128)S(1)}, f32[2,16,896]{2,1,0:T(8,128)S(1)}, u32[]{:S(2)}, u32[]{:S(2)}) collective-permute-start(f32[2,16,896]{2,1,0:T(8,128)S(1)} %get-tuple-element.52), channel_id=1, source_target_pairs={{0,4},{1,5},{2,6},{3,7},{4,0},{5,1},{6,2},{7,3},{8,12},{9,13},{10,... | collective-permute-start | bytes 344072 | tf_op jit(solution)/shard_map/ppermute | solution.py:347
  67.6 27.7 %collective-permute-start.13 = (bf16[2,2,56,512]{3,2,1,0:T(8,128)(2,1)S(1)}, bf16[2,2,56,512]{3,2,1,0:T(8,128)(2,1)S(1)}, u32[]{:S(2)}, u32[]{:S(2)}) collective-permute-start(bf16[2,2,56,512]{3,2,1,0:T(8,128)(2,1)S(1)} %collective-permute-done.12.refs_11_), channel_id=1, source_target_pairs={{0,8},{8,0},{16,24},{24,16},{32,40},{40,32},{48,56},{56,48},{64,72... | collective-permute-start | bytes 688136 | tf_op jit(solution)/shard_map/ppermute | solution.py:342
  68.3 27.0 %collective-permute-start.14 = (bf16[2,2,56,512]{3,2,1,0:T(8,128)(2,1)S(1)}, bf16[2,2,56,512]{3,2,1,0:T(8,128)(2,1)S(1)}, u32[]{:S(2)}, u32[]{:S(2)}) collective-permute-start(bf16[2,2,56,512]{3,2,1,0:T(8,128)(2,1)S(1)} %get-tuple-element.41), channel_id=1, source_target_pairs={{0,32},{8,40},{16,48},{24,56},{32,64},{40,72},{48,80},{56,88},{64,... | collective-permute-start | bytes 688136 | tf_op jit(solution)/shard_map/ppermute | solution.py:342
  71.1 24.2 %collective-permute-start.15 = (bf16[2,2,56,512]{3,2,1,0:T(8,128)(2,1)S(1)}, bf16[2,2,56,512]{3,2,1,0:T(8,128)(2,1)S(1)}, u32[]{:S(2)}, u32[]{:S(2)}) collective-permute-start(bf16[2,2,56,512]{3,2,1,0:T(8,128)(2,1)S(1)} %get-tuple-element.42), channel_id=1, source_target_pairs={{0,96},{8,104},{16,112},{24,120},{32,0},{40,8},{48,16},{56,24},{64... | collective-permute-start | bytes 688136 | tf_op jit(solution)/shard_map/ppermute | solution.py:342
  75.2 20.2 %collective-permute-start.16 = (bf16[2,2,56,512]{3,2,1,0:T(8,128)(2,1)S(1)}, bf16[2,2,56,512]{3,2,1,0:T(8,128)(2,1)S(1)}, u32[]{:S(2)}, u32[]{:S(2)}) collective-permute-start(bf16[2,2,56,512]{3,2,1,0:T(8,128)(2,1)S(1)} %get-tuple-element.43), channel_id=1, source_target_pairs={{0,16},{8,24},{16,32},{24,40},{32,48},{40,56},{48,64},{56,72},{64,... | collective-permute-start | bytes 688136 | tf_op jit(solution)/shard_map/ppermute | solution.py:342
  78.1 17.2 %collective-permute-start.17 = (bf16[2,2,56,512]{3,2,1,0:T(8,128)(2,1)S(1)}, bf16[2,2,56,512]{3,2,1,0:T(8,128)(2,1)S(1)}, u32[]{:S(2)}, u32[]{:S(2)}) collective-permute-start(bf16[2,2,56,512]{3,2,1,0:T(8,128)(2,1)S(1)} %get-tuple-element.44), channel_id=1, source_target_pairs={{0,112},{8,120},{16,0},{24,8},{32,16},{40,24},{48,32},{56,40},{64,... | collective-permute-start | bytes 688136 | tf_op jit(solution)/shard_map/ppermute | solution.py:342
